TPU v7x, 32 devices: a whole 2x2x4 slice. The times are simulated.
32 devices in a mesh: tok: 8 (over z, y), voc: 4 (over x, core).
Axes of the slice: x: 2, y: 2, z: 4, core: 2. Of those that a mesh axis runs over, the one named last changes fastest.
Arguments:
- hidden: bfloat16 [1024, 2048], P('tok'), may hold values from -6 to 6
- mix_weight: bfloat16 [4, 2048], P(None, 'voc'), may hold values from -0.0546875 to 0.0546875
- comp_proj: bfloat16 [2048, 4, 2048], P(None, None, 'voc'), may hold values from -0.110485435 to 0.110485435
- vocab_weight: bfloat16 [2048, 1024], P(None, 'voc'), may hold values from -0.625 to 0.625
- log_normalizer: float32 [4, 1024], P(None, 'tok'), may hold values from 11 to 11.6
- targets: int32 [1024], P('tok'), may hold values from 0 to 1023
- loss_grad: float32 [1024], P('tok'), may hold values from 0.5 to 1.5
Outputs:
- hidden_grad: bfloat16 [1024, 2048], P('tok', 'voc')
- proj_grad: bfloat16 [2048, 4, 2048], P('tok', None, 'voc')
- vocab_grad: bfloat16 [2048, 1024], P('tok', 'voc')
All inputs are finite; a program needn't handle non-finite values.
Results may differ from a plain program's by a relative error of at most 0.02.
Values may be sent and summed in bfloat16 or wider, within the bound.
A program may use at most 64 MiB of HBM per device.

v0:
```python
import functools

import jax
import jax.numpy as jnp
from jax import lax
from jax.experimental import pallas as pl
from jax.experimental.pallas import tpu as pltpu
from jax.sharding import PartitionSpec as P

MESH = pl.DeviceIdType.MESH
F32 = jnp.float32
BF16 = jnp.bfloat16
NT = (((1,), (1,)), ((), ()))
TN = (((0,), (0,)), ((), ()))


def column(row, lanes):
    wide = jnp.broadcast_to(row, (128, row.shape[1])).T
    return jnp.concatenate([wide] * (lanes // 128), axis=1)


def kernel(
    M, N,
    hidden, mix, proj_hbm, vw, logz, targets, loss,
    out_hidden, out_proj, out_vocab,
    w, ctx, mix_all, hblk, hrow, htr, logit, lg, tgt,
    cgs, cgr, cgx, xr, own_cg, vgb, vgy, vsum, vout, vin, pg, hss, hsr, own_hs, acc, psend, precv, mgrad,
    w_sem, ctx_s, ctx_f, ctx_r, mix_s, mix_r, hid_s, hid_r, tgt_s, tgt_r,
    cgp_s, cgp_r, cgx_s, cgx_r, vy_s, vy_r, vz_s, vz_r, hs_s, hs_r, ag_s, ag_r, pp_s, pp_r,
):
    K, D, E = w.shape
    T = hidden.shape[0]
    V = vw.shape[1]
    R = D // M
    half = N // 2
    Z = M // 2
    me_t = lax.axis_index("tok")
    me_v = lax.axis_index("voc")
    chip = me_v // 2
    core = me_v % 2
    partner = me_v + 1 - 2 * core
    z = me_t // 2
    y = me_t % 2
    ypart = me_t + 1 - 2 * y
    sends = []

    def remote(src, dst, ss, rs, dev):
        return pltpu.make_async_remote_copy(
            src_ref=src, dst_ref=dst, send_sem=ss, recv_sem=rs,
            device_id=dev, device_id_type=MESH,
        )

    def send(src, dst, ss, rs, dev):
        c = remote(src, dst, ss, rs, dev)
        c.start()
        sends.append((None, c))

    def arrived(ref, rs, ss):
        remote(ref, ref, ss, rs, {"voc": partner}).wait_recv()

    for k in range(K):
        pltpu.make_async_copy(proj_hbm.at[k], w.at[k], w_sem.at[k]).start()
    for j in range(M):
        hblk[j // 2, j % 2] = hidden[:, j * R:(j + 1) * R]

    bar = pltpu.get_barrier_semaphore()
    for d in range(1, M):
        pl.semaphore_signal(bar, inc=1, device_id={"tok": lax.rem(me_t + d, M)}, device_id_type=MESH)
    for d in range(1, N):
        pl.semaphore_signal(bar, inc=1, device_id={"voc": lax.rem(me_v + d, N)}, device_id_type=MESH)
    pl.semaphore_wait(bar, M + N - 2)

    for d in range(1, N):
        send(mix, mix_all.at[d], mix_s.at[d], mix_r.at[d], {"voc": lax.rem(me_v + d, N)})
    mix_all[0] = mix[...]
    for d in range(1, Z):
        zz = lax.rem(z + d, Z)
        send(hblk.at[zz], hrow.at[:, pl.ds(z * T, T)], hid_s.at[d], hid_r.at[d],
             {"tok": zz * 2 + y})
    hrow[:, rows_of(z, T), :] = hblk[z]

    for k in range(K):
        pltpu.make_async_copy(proj_hbm.at[k], w.at[k], w_sem.at[k]).wait()
        ctx[me_v, k * T:(k + 1) * T, :] = jnp.tanh(
            jnp.dot(hidden[...], w[k], preferred_element_type=F32)
        ).astype(BF16)
        piece = ctx.at[me_v, pl.ds(k * T, T)]
        for i in range(1, half):
            send(piece, piece, ctx_s.at[i, k], ctx_r.at[me_v, k],
                 {"voc": lax.rem(chip + i, half) * 2 + core})
        send(piece, piece, ctx_s.at[0, k], ctx_r.at[me_v, k], {"voc": partner})

    def add_logits(s, first=False):
        part = jnp.dot(ctx[s], vw[pl.ds(pl.multiple_of(s * E, E), E), :],
                       preferred_element_type=F32)
        logit[...] = part if first else logit[...] + part

    add_logits(me_v, True)
    for k in range(K):
        arrived(ctx.at[partner, pl.ds(k * T, T)], ctx_r.at[partner, k], ctx_s.at[0, k])
    add_logits(partner)

    tcol = column(targets[...].astype(F32), V)
    ids = (me_v * V + lax.broadcasted_iota(jnp.int32, (T, V), 1)).astype(F32)
    onehot = (tcol == ids).astype(F32)
    for d in range(1, N):
        arrived(mix_all.at[d], mix_r.at[d], mix_s.at[d])
    mixing = jnp.zeros((K, T), F32)
    for d in range(N):
        s = lax.rem(me_v - d + N, N)
        mixing = mixing + lax.dot_general(
            mix_all[d], hidden[:, pl.ds(pl.multiple_of(s * E, E), E)], NT,
            preferred_element_type=F32)
    exp_mix = jnp.exp(mixing)
    weights = exp_mix / jnp.sum(exp_mix, axis=0, keepdims=True)

    for i in range(1, half):
        s = lax.rem(chip - i + half, half) * 2 + core
        for k in range(K):
            piece = ctx.at[s, pl.ds(k * T, T)]
            arrived(piece, ctx_r.at[s, k], ctx_s.at[i, k])
            send(piece, piece, ctx_f.at[i, k], ctx_r.at[s, k], {"voc": partner})
        add_logits(s)
    for i in range(1, half):
        s = lax.rem(chip - i + half, half) * 2 + 1 - core
        for k in range(K):
            arrived(ctx.at[s, pl.ds(k * T, T)], ctx_r.at[s, k], ctx_s.at[i, k])
        add_logits(s)

    lane = lax.broadcasted_iota(jnp.int32, (T, 128), 1)
    table = jnp.zeros((T, 128), F32)
    for k in range(K):
        part = jnp.sum(logit[k * T:(k + 1) * T, :] * onehot, axis=1, keepdims=True)
        table = jnp.where(lane == k, part, table)
    tgt[0] = table.T[0:8, :]
    for d in range(1, N):
        send(tgt.at[0], tgt.at[d], tgt_s.at[d], tgt_r.at[d], {"voc": lax.rem(me_v + d, N)})
    for k in range(K):
        rows = slice(k * T, (k + 1) * T)
        logit[rows, :] = jnp.exp(logit[rows, :] - column(logz[k:k + 1, :], V)) - onehot
    for d in range(1, N):
        arrived(tgt.at[d], tgt_r.at[d], tgt_s.at[d])
    target = tgt[0]
    for d in range(1, N):
        target = target + tgt[d]
    likely = jnp.exp(target[0:K, :] - logz[...])
    joint = weights * likely
    posterior = joint / jnp.sum(joint, axis=0, keepdims=True)
    factor = loss[...] * posterior
    mgrad[...] = loss[...] * (weights - posterior)
    for k in range(K):
        rows = slice(k * T, (k + 1) * T)
        lg[rows, :] = (column(factor[k:k + 1, :], V) * logit[rows, :]).astype(BF16)

    def cg_part(s, k):
        return lax.dot_general(
            lg[k * T:(k + 1) * T, :], vw[pl.ds(pl.multiple_of(s * E, E), E), :], NT,
            preferred_element_type=F32)

    for i in list(range(1, half)) + [0]:
        s = lax.rem(chip + i, half) * 2
        for k in range(K):
            cgs[i, k] = cg_part(s + 1 - core, k).astype(BF16)
            send(cgs.at[i, k], cgr.at[i, k], cgp_s.at[i, k], cgp_r.at[i, k], {"voc": partner})
        for k in range(K):
            part = cg_part(s + core, k)
            if i == 0:
                own_cg[k] = part
            else:
                arrived(cgr.at[i, k], cgp_r.at[i, k], cgp_s.at[i, k])
                cgx[i, k] = (part + cgr[i, k].astype(F32)).astype(BF16)
                send(cgx.at[i, k], xr.at[i, k], cgx_s.at[i, k], cgx_r.at[i, k], {"voc": s + core})

    for s in range(N):
        vgb[s * E:(s + 1) * E, :] = lax.dot_general(
            ctx[s], lg[...], TN, preferred_element_type=F32).astype(BF16)
    for zz in range(Z):
        send(vgb.at[pl.ds((zz * 2 + 1 - y) * R, R)], vgy.at[zz], vy_s.at[zz], vy_r.at[zz],
             {"tok": ypart})

    for d in range(1, Z):
        src = lax.rem(z - d + Z, Z)
        arrived(hrow.at[:, pl.ds(src * T, T)], hid_r.at[d], hid_s.at[d])
    for b in range(2):
        htr[b] = hrow[b].T

    pieces = [(k, 0, E) for k in range(K)]
    if E % 256 == 0:
        pieces[-1:] = [(K - 1, 0, E // 2), (K - 1, E // 2, E // 2)]

    def relay(t, p, way, pred):
        k, lo, wide = pieces[p]
        piece = pg.at[k, rows_of(t, T), pl.ds(lo, wide)]
        c = remote(piece, piece, ag_s.at[way, t, p], ag_r.at[t, p],
                   {"tok": me_t + 2 - 4 * way})
        pl.when(pred)(c.start)
        sends.append((pred, c))

    has_r = z + 1 < Z
    has_l = z >= 1
    for k in range(K):
        total = own_cg[k]
        arrived(cgr.at[0, k], cgp_r.at[0, k], cgp_s.at[0, k])
        total = total + cgr[0, k].astype(F32)
        for i in range(1, half):
            arrived(xr.at[i, k], cgx_r.at[i, k], cgx_s.at[i, k])
            total = total + xr[i, k].astype(F32)
        c = ctx[me_v, k * T:(k + 1) * T, :].astype(F32)
        pg[k, rows_of(z, T), :] = (total * (1.0 - c * c)).astype(BF16)
        if Z > 1:
            for p in range(len(pieces)):
                if pieces[p][0] == k:
                    relay(z, p, 0, has_r)
                    relay(z, p, 1, has_l)

    def hid_part(s):
        total = jnp.zeros((T, E), F32)
        for k in range(K):
            total = total + lax.dot_general(
                pg[k, rows_of(z, T), :], w[k, pl.ds(pl.multiple_of(s * E, E), E), :], NT,
                preferred_element_type=F32)
        return total

    def hid_send(d):
        s = lax.rem(me_v + d, N)
        if d == 0:
            own_hs[...] = hid_part(s)
        else:
            hss[d] = hid_part(s).astype(BF16)
            send(hss.at[d], hsr.at[d], hs_s.at[d], hs_r.at[d], {"voc": s})

    hid_order = list(range(1, N)) + [0]
    hid_per = -(-N // (len(pieces) - 1))

    def pair_sums():
        for zz in range(Z):
            arrived(vgy.at[zz], vy_r.at[zz], vy_s.at[zz])
            vsum[zz] = vgb[rows_of(zz * 2 + y, R), :].astype(F32) + vgy[zz].astype(F32)

    def hop(h):
        for way, at, ends in ((0, h, range(h + 1, Z)), (1, Z - 1 - h, range(Z - 1 - h))):
            copies = [
                remote(vout.at[way, e], vin.at[way, e], vz_s.at[way, e], vz_r.at[way, e],
                       {"tok": me_t + 2 - 4 * way})
                for e in ends
            ]

            @pl.when(z == at)
            def _(way=way, ends=ends, copies=copies):
                for e, c in zip(ends, copies):
                    part = vsum[e]
                    if h > 0:
                        arrived(vin.at[way, e], vz_r.at[way, e], vz_s.at[way, e])
                        part = part + vin[way, e].astype(F32)
                    vout[way, e] = part.astype(BF16)
                    c.start()
            for c in copies:
                sends.append((z == at, c))

    if Z == 1:
        for e in hid_order:
            hid_send(e)
    per = -(-(Z - 1) // (len(pieces) - 1))
    for p, (k, lo, wide) in enumerate(pieces):
        lanes = slice(lo, lo + wide)
        for d in range(1, Z):
            for there, t, way, more in (
                (z >= d, z - d, 0, has_r), (z + d < Z, z + d, 1, has_l),
            ):
                def _(t=t):
                    arrived(pg.at[k, rows_of(t, T), pl.ds(lo, wide)], ag_r.at[t, p], ag_s.at[0, t, p])
                pl.when(there)(_)
                if d < Z - 1:
                    relay(t, p, way, there & more)
            if d == 1:
                for e in hid_order[p * hid_per:(p + 1) * hid_per]:
                    hid_send(e)
        psend[k, :, lanes] = jnp.dot(
            htr[1 - y], pg[k, :, lanes], preferred_element_type=F32).astype(BF16)
        send(psend.at[k, :, pl.ds(lo, wide)], precv.at[k, :, pl.ds(lo, wide)],
             pp_s.at[p], pp_r.at[p], {"tok": ypart})
        acc[k, :, lanes] = jnp.dot(htr[y], pg[k, :, lanes], preferred_element_type=F32)
        if p == 0:
            pair_sums()
        for h in range(p * per, min((p + 1) * per, Z - 1)):
            hop(h)

    acc_v = vsum.at[z]
    for way, pred in ((0, has_l), (1, has_r)):
        @pl.when(pred)
        def _(way=way):
            arrived(vin.at[way, z], vz_r.at[way, z], vz_s.at[way, z])
            acc_v[...] += vin[way, z].astype(F32)
    out_vocab[...] = acc_v[...].astype(BF16)
    htot = own_hs[...]
    for d in range(1, N):
        arrived(hsr.at[d], hs_r.at[d], hs_s.at[d])
        htot = htot + hsr[d].astype(F32)
    mixf = mix[...].astype(F32)
    for k in range(K):
        htot = htot + column(mgrad[k:k + 1, :], E) * mixf[k:k + 1, :]
    out_hidden[...] = htot.astype(BF16)

    for p, (k, lo, wide) in enumerate(pieces):
        lanes = slice(lo, lo + wide)
        arrived(precv.at[k, :, pl.ds(lo, wide)], pp_r.at[p], pp_s.at[p])
        out_proj[k, :, lanes] = (acc[k, :, lanes] + precv[k, :, lanes].astype(F32)).astype(BF16)
    for pred, c in sends:
        if pred is None:
            c.wait_send()
        else:
            pl.when(pred)(c.wait_send)


def rows_of(block, size):
    return pl.ds(pl.multiple_of(block * size, size), size)


def body(M, N, hidden, mix_weight, comp_proj, vocab_weight, log_normalizer, targets, loss_grad):
    T, D = hidden.shape
    K, E = mix_weight.shape
    V = vocab_weight.shape[1]
    R = D // M
    half = N // 2
    Z = M // 2
    w = jnp.transpose(comp_proj, (1, 0, 2))
    vm = pltpu.VMEM
    dma = pltpu.SemaphoreType.DMA
    scratch = [
        vm((K, D, E), BF16), vm((N, K * T, E), BF16), vm((N, K, E), BF16),
        vm((Z, 2, T, R), BF16), vm((2, Z * T, R), BF16), vm((2, R, Z * T), BF16), vm((K * T, V), F32), vm((K * T, V), BF16),
        vm((N, 8, T), F32),
        vm((half, K, T, E), BF16), vm((half, K, T, E), BF16),
        vm((half, K, T, E), BF16), vm((half, K, T, E), BF16),
        vm((K, T, E), F32), vm((D, V), BF16), vm((Z, R, V), BF16),
        vm((Z, R, V), F32), vm((2, Z, R, V), BF16), vm((2, Z, R, V), BF16),
        vm((K, Z * T, E), BF16), vm((N, T, E), BF16), vm((N, T, E), BF16),
        vm((T, E), F32), vm((K, R, E), F32), vm((K, R, E), BF16), vm((K, R, E), BF16),
        vm((K, T), F32),
        dma((K,)), dma((half, K)), dma((half, K)), dma((N, K)), dma((N,)), dma((N,)),
        dma((Z,)), dma((Z,)), dma((N,)), dma((N,)),
        dma((half, K)), dma((half, K)), dma((half, K)), dma((half, K)),
        dma((Z,)), dma((Z,)), dma((2, Z)), dma((2, Z)), dma((N,)), dma((N,)),
        dma((2, Z, K + 1)), dma((Z, K + 1)), dma((K + 1,)), dma((K + 1,)),
    ]
    spec = pl.BlockSpec(memory_space=pltpu.VMEM)
    hidden_grad, proj_grad, vocab_grad = pl.pallas_call(
        functools.partial(kernel, M, N),
        out_shape=(
            jax.ShapeDtypeStruct((T, E), BF16),
            jax.ShapeDtypeStruct((K, R, E), BF16),
            jax.ShapeDtypeStruct((R, V), BF16),
        ),
        in_specs=[spec, spec, pl.BlockSpec(memory_space=pltpu.MemorySpace.HBM)] + [spec] * 4,
        out_specs=(spec, spec, spec),
        scratch_shapes=scratch,
        compiler_params=pltpu.CompilerParams(
            collective_id=0, has_side_effects=True, vmem_limit_bytes=48 * 1024 * 1024
        ),
    )(hidden, mix_weight, w, vocab_weight, log_normalizer, targets[None, :], loss_grad[None, :])
    return hidden_grad, jnp.transpose(proj_grad, (1, 0, 2)), vocab_grad


def solution(mesh):
    in_specs = (
        P("tok", None),
        P(None, "voc"),
        P(None, None, "voc"),
        P(None, "voc"),
        P(None, "tok"),
        P("tok"),
        P("tok"),
    )
    out_specs = (P("tok", "voc"), P("tok", None, "voc"), P("tok", "voc"))
    return jax.shard_map(
        functools.partial(body, mesh.shape["tok"], mesh.shape["voc"]),
        mesh=mesh, in_specs=in_specs, out_specs=out_specs, check_vma=False,
    )
```

profile of v0, /device:TPU:0, one launch (start us, length us, event | category | flops | bytes accessed | tf_op | source)
XLA Modules:
  0.0 92.4 jit_solution(4988675896676467432)
XLA Ops:
  0.6 0.0 copy-start
  0.6 0.0 copy-start.1
  0.7 0.0 copy-start.2
  0.7 0.0 copy-start.3
  0.7 0.0 copy-start.4
  0.7 0.0 copy-start.5
  0.7 8.4 %copy.13 = bf16[2048,4,512]{2,0,1:T(8,128)(2,1)} copy(bf16[2048,4,512]{2,1,0:T(4,128)(2,1)} %param.9) | data formatting | bytes 16777216 | tf_op args[2]
  9.1 0.0 copy-done
  9.1 0.0 copy-done.1
  9.1 0.0 copy-done.2
  9.1 0.0 copy-done.3
  9.1 0.0 copy-done.4
  9.1 0.0 copy-done.5
  9.1 80.2 %shard_map.94 = (bf16[128,512]{1,0:T(8,128)(2,1)S(1)}, bf16[4,256,512]{2,1,0:T(8,128)(2,1)S(1)}, bf16[256,256]{1,0:T(8,128)(2,1)S(1)}) custom-call(bf16[128,2048]{1,0:T(8,128)(2,1)S(1)} %copy-done.1, bf16[4,512]{1,0:T(4,128)(2,1)S(1)} %copy-done.2, bf16[4,2048,512]{2,1,0:T(8,128)(2,1)} %bitcast.9, bf16[2048,256]{1,0:T(8,128)(2,1)S(1)} %copy-done, ...), custom_call_target="tpu_custom_call" | custom-call | tf_op jit(solution)/shard_map/pallas_call | solution.py:347
  89.3 1.8 %copy.11 = bf16[256,4,512]{2,1,0:T(4,128)(2,1)} copy(bf16[256,4,512]{2,0,1:T(8,128)(2,1)S(1)} %bitcast.6) | data formatting | bytes 2097152
  91.1 0.7 copy.16
  91.8 0.7 copy.17
Async XLA Ops:
  0.6 8.5 %copy-start = (bf16[2048,256]{1,0:T(8,128)(2,1)S(1)}, bf16[2048,256]{1,0:T(8,128)(2,1)}, u32[]{:S(2)}) copy-start(bf16[2048,256]{1,0:T(8,128)(2,1)} %vw.1) | copy-start | bytes 3145732
  0.6 8.5 %copy-start.1 = (bf16[128,2048]{1,0:T(8,128)(2,1)S(1)}, bf16[128,2048]{1,0:T(8,128)(2,1)}, u32[]{:S(2)}) copy-start(bf16[128,2048]{1,0:T(8,128)(2,1)} %hidden.1) | copy-start | bytes 1572868
  0.7 8.5 %copy-start.2 = (bf16[4,512]{1,0:T(4,128)(2,1)S(1)}, bf16[4,512]{1,0:T(4,128)(2,1)}, u32[]{:S(2)}) copy-start(bf16[4,512]{1,0:T(4,128)(2,1)} %mix.1) | copy-start | bytes 12292
  0.7 8.5 %copy-start.3 = (f32[4,128]{1,0:T(4,128)S(1)}, f32[4,128]{1,0:T(4,128)}, u32[]{:S(2)}) copy-start(f32[4,128]{1,0:T(4,128)} %logz.1) | copy-start | bytes 6148
  0.7 8.5 %copy-start.4 = (s32[128]{0:T(128)S(1)}, s32[128]{0:T(128)}, u32[]{:S(2)}) copy-start(s32[128]{0:T(128)} %param.12) | copy-start | bytes 1540
  0.7 8.5 %copy-start.5 = (f32[128]{0:T(128)S(1)}, f32[128]{0:T(128)}, u32[]{:S(2)}) copy-start(f32[128]{0:T(128)} %param.13) | copy-start | bytes 1540
where the time goes:
time: 92.6 us; the launch traced here: 92.4 us
  Pallas kernels  80.2 us (87%)
  local copies, waits for them, and re-layouts  11.5 us (12%)
    pallas_call x1, Pallas kernels, body(): pl.pallas_call(functools.partial(kernel, M, N), out_shape=(jax.ShapeDtype...  80.2 us
    unnamed x16, local copies, waits for them, and re-layouts  11.5 us

commit v1 on v0

--- a/solution.py
+++ b/solution.py
@@ -316,7 +316,7 @@
     return pl.ds(pl.multiple_of(block * size, size), size)
 
 
-def body(M, N, hidden, mix_weight, comp_proj, vocab_weight, log_normalizer, targets, loss_grad):
+def body_base(M, N, hidden, mix_weight, comp_proj, vocab_weight, log_normalizer, targets, loss_grad):
     T, D = hidden.shape
     K, E = mix_weight.shape
     V = vocab_weight.shape[1]
@@ -361,6 +361,621 @@
     return hidden_grad, jnp.transpose(proj_grad, (1, 0, 2)), vocab_grad
 
 
+def scoped(fn):
+    def run(*args, **kw):
+        tag = "_".join(str(a) for a in args if isinstance(a, int))
+        with jax.named_scope(fn.__name__ + "_" + tag):
+            return fn(*args, **kw)
+    return run
+
+
+def mix_rows(K, flip=False):
+    B = 256 // K
+    r = lax.broadcasted_iota(jnp.int32, (256, 256), 1 if flip else 0)
+    c = lax.broadcasted_iota(jnp.int32, (256, 256), 0 if flip else 1)
+    return (c == K * (r % B) + r // B).astype(F32).astype(BF16)
+
+
+def fast_kernel(
+    M, N,
+    hid_hbm, mix_hbm, proj_hbm, vw_hbm, logz_hbm, tg_hbm, loss_hbm,
+    out_hidden, out_proj, out_vocab,
+    raw, w, hida, vw, vwe, vwt, mix, logz, targets, loss,
+    ctx, ctxz, mix_all, htr, logit, lgall, tgt, pg,
+    vgb, vgy, vsum, vout, vin, hss, hsr, own_hs, acc, psend, precv, mgrad,
+    l_sem, w_sem, ctx_s, ctx_f, ctx_r, mix_s, mix_r, hz_s, hz_r, hp_s, hp_r,
+    vx_s, vx_r, vp_s, vp_r, vwz_s, vwy_s, vw_r, tgt_s, tgt_r,
+    lz_s, lx_s, lp_s, lg_r, vy_s, vy_r, vz_s, vz_r, hs_s, hs_r, pp_s, pp_r,
+):
+    K, D, E = w.shape
+    T = hida.shape[2]
+    H = D // 2
+    V = vw.shape[1]
+    R = D // M
+    J = E // 128
+    S = E // M
+    half = N // 2
+    Z = M // 2
+    B = 256 // K
+    me_t = lax.axis_index("tok")
+    me_v = lax.axis_index("voc")
+    chip = me_v // 2
+    core = me_v % 2
+    partner = me_v + 1 - 2 * core
+    z = me_t // 2
+    y = me_t % 2
+    ypart = me_t + 1 - 2 * y
+    has_r = z + 1 < Z
+    has_l = z >= 1
+    sends = []
+
+    def remote(src, dst, ss, rs, dev):
+        return pltpu.make_async_remote_copy(
+            src_ref=src, dst_ref=dst, send_sem=ss, recv_sem=rs,
+            device_id=dev, device_id_type=MESH,
+        )
+
+    def send(src, dst, ss, rs, dev, pred=None):
+        c = remote(src, dst, ss, rs, dev)
+        if pred is None:
+            c.start()
+        else:
+            pl.when(pred)(c.start)
+        sends.append((pred, c))
+
+    def arrived(ref, rs, ss):
+        remote(ref, ref, ss, rs, {"voc": partner}).wait_recv()
+
+    def mate(j):
+        if j == 0:
+            return z
+        near = jnp.minimum(z, Z - 1 - z)
+        d = (j + 1) // 2
+        both = z + d if j % 2 == 1 else z - d
+        return jnp.where(j <= 2 * near, both, jnp.where(2 * z < Z, j, Z - 1 - j))
+
+    def onward(zz):
+        right = zz < z
+        there = (right & has_r) | (jnp.logical_not(right) & has_l)
+        return there, me_t + jnp.where(right, 2, -2)
+
+    chunks = 4
+    n = D // chunks
+
+    def w_copy(c, j):
+        return pltpu.make_async_copy(
+            proj_hbm.at[pl.ds(c * n, n), :, pl.ds(j * 128, 128)],
+            raw.at[j, pl.ds(c * n, n)], w_sem.at[c, j])
+
+    loads = [
+        pltpu.make_async_copy(hid_hbm.at[:, pl.ds(0, H)], hida.at[z, 0], l_sem.at[0]),
+        pltpu.make_async_copy(hid_hbm.at[:, pl.ds(H, H)], hida.at[z, 1], l_sem.at[1]),
+        pltpu.make_async_copy(vw_hbm, vw, l_sem.at[2]),
+        pltpu.make_async_copy(mix_hbm, mix, l_sem.at[3]),
+        pltpu.make_async_copy(logz_hbm, logz, l_sem.at[4]),
+        pltpu.make_async_copy(tg_hbm, targets, l_sem.at[5]),
+        pltpu.make_async_copy(loss_hbm, loss, l_sem.at[6]),
+    ]
+    for c in loads:
+        c.start()
+
+    bar = pltpu.get_barrier_semaphore()
+    for d in range(1, M):
+        pl.semaphore_signal(bar, inc=1, device_id={"tok": lax.rem(me_t + d, M)}, device_id_type=MESH)
+    for d in range(1, N):
+        pl.semaphore_signal(bar, inc=1, device_id={"voc": lax.rem(me_v + d, N)}, device_id_type=MESH)
+
+    perm = mix_rows(K)
+
+    @scoped
+    def unmix(c):
+        for j in range(J):
+            w_copy(c, j).wait()
+        for b in range(c * n // B, (c + 1) * n // B):
+            x = jnp.concatenate(
+                [raw.at[j].reshape(D * K, 128)[b * 256:(b + 1) * 256, :] for j in range(J)], axis=1)
+            rows = jnp.dot(perm, x, preferred_element_type=F32).astype(BF16)
+            for k in range(K):
+                w[k, b * B:(b + 1) * B, :] = rows[k * B:(k + 1) * B]
+
+    with jax.named_scope("loads"):
+        for c in loads[:3]:
+            c.wait()
+    for c in range(chunks):
+        for j in range(J):
+            w_copy(c, j).start()
+    with jax.named_scope("barrier"):
+        pl.semaphore_wait(bar, M + N - 2)
+
+    def vw_piece(ci, t):
+        return vwe.at[pl.ds(ci * 2, 2), rows_of(t, S)]
+
+    @scoped
+    def vw_own():
+        for i in range(1, half):
+            ci = lax.rem(chip + i, half)
+            for c in range(2):
+                arrived(vwe.at[ci * 2 + c, rows_of(me_t, S)], vx_r.at[ci * 2 + c], vx_s.at[i, c])
+            piece = vw_piece(ci, me_t)
+            send(piece, piece, vwy_s.at[i, z], vw_r.at[ci, me_t], {"tok": ypart})
+            for d in range(1, Z):
+                send(piece, piece, vwz_s.at[i, d], vw_r.at[ci, me_t], {"tok": lax.rem(me_t + 2 * d, M)})
+
+    def slab(v, t):
+        return pl.ds(pl.multiple_of(v * E + t * S, S), S)
+
+    for i in range(1, half):
+        for c in range(2):
+            v = lax.rem(chip + i, half) * 2 + c
+            send(vw.at[slab(v, me_t)], vwe.at[me_v, rows_of(me_t, S)],
+                 vx_s.at[i, c], vx_r.at[me_v], {"voc": v})
+    send(hida.at[z, core], hida.at[z, core], hz_s.at[0, z], hz_r.at[z], {"tok": me_t + 2}, has_r)
+    send(hida.at[z, core], hida.at[z, core], hz_s.at[1, z], hz_r.at[z], {"tok": me_t - 2}, has_l)
+    for c in loads[3:]:
+        c.wait()
+    for d in range(1, N):
+        send(mix, mix_all.at[d], mix_s.at[d], mix_r.at[d], {"voc": lax.rem(me_v + d, N)})
+    send(vw.at[rows_of(partner, E)], vwe.at[me_v], vp_s.at[0], vp_r.at[0], {"voc": partner})
+    for c in range(chunks):
+        unmix(c)
+    vw_own()
+
+    def context(zz, k):
+        both = jnp.dot(hida[zz, 0], w[k, 0:H, :], preferred_element_type=F32)
+        both = both + jnp.dot(hida[zz, 1], w[k, H:D, :], preferred_element_type=F32)
+        return jnp.tanh(both).astype(BF16)
+
+    for k in range(K):
+        with jax.named_scope("context"):
+            ctx[me_v, k * T:(k + 1) * T, :] = context(z, k)
+        piece = ctx.at[me_v, pl.ds(k * T, T)]
+        for i in range(1, half):
+            send(piece, piece, ctx_s.at[i, k], ctx_r.at[me_v, k],
+                 {"voc": lax.rem(chip + i, half) * 2 + core})
+        send(piece, piece, ctx_s.at[0, k], ctx_r.at[me_v, k], {"voc": partner})
+
+    @scoped
+    def add_logits(s, first=False):
+        part = jnp.dot(ctx[s], vw[rows_of(s, E), :], preferred_element_type=F32)
+        logit[...] = part if first else logit[...] + part
+
+    @scoped
+    def relay_vw(j):
+        zz = mate(j)
+        t = zz * 2 + y
+        for i in range(1, half):
+            ci = lax.rem(chip + i, half)
+            piece = vw_piece(ci, t)
+            arrived(piece, vw_r.at[ci, t], vwy_s.at[i, zz])
+            send(piece, piece, vwy_s.at[i, zz], vw_r.at[ci, t], {"tok": ypart})
+
+    @scoped
+    def relay_hid(j, fwd):
+        zz = mate(j)
+        there, to = onward(zz)
+        piece = hida.at[zz, core]
+        on = remote(piece, piece, hz_s.at[0, zz], hz_r.at[zz], {"tok": to})
+        over = remote(piece, piece, hp_s.at[zz], hp_r.at[zz], {"voc": partner})
+
+        @pl.when(there if fwd else jnp.logical_not(there))
+        def _():
+            arrived(piece, hz_r.at[zz], hz_s.at[0, zz])
+            if fwd:
+                on.start()
+            over.start()
+        if fwd:
+            sends.append((there, on))
+            sends.append((None, over))
+
+    @scoped
+    def ctx_mate(j, ks):
+        zz = mate(j)
+        if ks[0] == 0:
+            arrived(hida.at[zz, 1 - core], hp_r.at[zz], hp_s.at[zz])
+        for k in ks:
+            ctxz[zz, k * T:(k + 1) * T, :] = context(zz, k)
+
+    @scoped
+    def ctx_pass(k):
+        for i in range(1, half):
+            s = lax.rem(chip - i + half, half) * 2 + core
+            piece = ctx.at[s, pl.ds(k * T, T)]
+            arrived(piece, ctx_r.at[s, k], ctx_s.at[i, k])
+            send(piece, piece, ctx_f.at[i, k], ctx_r.at[s, k], {"voc": partner})
+
+    add_logits(me_v, True)
+    for k in range(K):
+        arrived(ctx.at[partner, pl.ds(k * T, T)], ctx_r.at[partner, k], ctx_s.at[0, k])
+    add_logits(partner)
+
+    tcol = column(targets[...].astype(F32), V)
+    ids = (me_v * V + lax.broadcasted_iota(jnp.int32, (T, V), 1)).astype(F32)
+    onehot = (tcol == ids).astype(F32)
+    mix_all[0] = mix[...]
+    for d in range(1, N):
+        arrived(mix_all.at[d], mix_r.at[d], mix_s.at[d])
+    mixing = jnp.zeros((K, T), F32)
+    for d in range(N):
+        s = lax.rem(me_v - d + N, N)
+        mixing = mixing + lax.dot_general(
+            mix_all[d],
+            hida[z, s // half, :, pl.ds(pl.multiple_of((s % half) * E, E), E)], NT,
+            preferred_element_type=F32)
+    exp_mix = jnp.exp(mixing)
+    weights = exp_mix / jnp.sum(exp_mix, axis=0, keepdims=True)
+
+    ctx_pass(0)
+    for j in range(1, min(Z, 3)):
+        relay_hid(j, True)
+    if Z > 1:
+        relay_hid(1, False)
+    ctx_pass(1)
+    for j in range(1, Z):
+        relay_vw(j)
+    if Z > 1:
+        ctx_mate(1, range(K))
+    for k in range(2, K):
+        ctx_pass(k)
+    for i in range(1, half):
+        add_logits(lax.rem(chip - i + half, half) * 2 + core)
+    for i in range(1, half):
+        s = lax.rem(chip - i + half, half) * 2 + 1 - core
+        for k in range(K):
+            arrived(ctx.at[s, pl.ds(k * T, T)], ctx_r.at[s, k], ctx_s.at[i, k])
+        add_logits(s)
+
+    lane = lax.broadcasted_iota(jnp.int32, (T, 128), 1)
+    table = jnp.zeros((T, 128), F32)
+    for k in range(K):
+        part = jnp.sum(logit[k * T:(k + 1) * T, :] * onehot, axis=1, keepdims=True)
+        table = jnp.where(lane == k, part, table)
+    tgt[0] = table.T[0:8, :]
+    for d in range(1, N):
+        send(tgt.at[0], tgt.at[d], tgt_s.at[d], tgt_r.at[d], {"voc": lax.rem(me_v + d, N)})
+    for j in range(3, Z):
+        relay_hid(j, True)
+    if Z > 2:
+        relay_hid(2, False)
+    for k in range(K):
+        rows = slice(k * T, (k + 1) * T)
+        logit[rows, :] = jnp.exp(logit[rows, :] - column(logz[k:k + 1, :], V)) - onehot
+    with jax.named_scope("targets"):
+        for d in range(1, N):
+            arrived(tgt.at[d], tgt_r.at[d], tgt_s.at[d])
+    target = tgt[0]
+    for d in range(1, N):
+        target = target + tgt[d]
+    likely = jnp.exp(target[0:K, :] - logz[...])
+    joint = weights * likely
+    posterior = joint / jnp.sum(joint, axis=0, keepdims=True)
+    factor = loss[...] * posterior
+    mgrad[...] = loss[...] * (weights - posterior)
+
+    def shares(zz, k):
+        piece = lgall.at[zz, me_v, k]
+        return [
+            remote(piece, piece, lx_s.at[i, zz, k], lg_r.at[zz, me_v, k],
+                   {"voc": lax.rem(chip + i, half) * 2 + core})
+            for i in range(1, half)
+        ] + [remote(piece, piece, lp_s.at[0, zz, k], lg_r.at[zz, me_v, k], {"voc": partner})]
+
+    def share(zz, k):
+        for c in shares(zz, k):
+            c.start()
+            sends.append((None, c))
+
+    def fill(ks):
+        for k in ks:
+            rows = slice(k * T, (k + 1) * T)
+            lgall[z, me_v, k] = (column(factor[k:k + 1, :], V) * logit[rows, :]).astype(BF16)
+
+    @scoped
+    def own_out(k):
+        if k < 2:
+            fill(range(K)[k:] if k else range(1))
+        piece = lgall.at[z, me_v, k]
+        send(piece, piece, lz_s.at[0, z, k], lg_r.at[z, me_v, k], {"tok": me_t + 2}, has_r)
+        send(piece, piece, lz_s.at[1, z, k], lg_r.at[z, me_v, k], {"tok": me_t - 2}, has_l)
+        share(z, k)
+
+    @scoped
+    def relay_lg(k, j, fwd):
+        zz = mate(j)
+        there, to = onward(zz)
+        piece = lgall.at[zz, me_v, k]
+        on = remote(piece, piece, lz_s.at[0, zz, k], lg_r.at[zz, me_v, k], {"tok": to})
+
+        @pl.when(there if fwd else jnp.logical_not(there))
+        def _():
+            arrived(piece, lg_r.at[zz, me_v, k], lp_s.at[0, zz, k])
+            if fwd:
+                on.start()
+            for c in shares(zz, k):
+                c.start()
+        if fwd:
+            sends.append((there, on))
+            for c in shares(zz, k):
+                sends.append((None, c))
+
+    @scoped
+    def cross_lg(k, j):
+        zz = mate(j)
+        for i in range(1, half):
+            s = lax.rem(chip - i + half, half) * 2 + core
+            piece = lgall.at[zz, s, k]
+            arrived(piece, lg_r.at[zz, s, k], lp_s.at[0, zz, k])
+            send(piece, piece, lp_s.at[i, zz, k], lg_r.at[zz, s, k], {"voc": partner})
+
+    @scoped
+    def pre_grad(k, j):
+        zz = mate(j)
+        rows = slice(k * T, (k + 1) * T)
+        for i in range(half):
+            s = lax.rem(chip + i, half) * 2 + 1 - core
+            arrived(lgall.at[zz, s, k], lg_r.at[zz, s, k], lp_s.at[0, zz, k])
+        total = None
+        for s in range(N):
+            part = jnp.dot(lgall[zz, s, k], vwt[s], preferred_element_type=F32)
+            total = part if total is None else total + part
+        c = (ctx[me_v, rows, :] if j == 0 else ctxz[zz, rows, :]).astype(F32)
+        pg[k, rows_of(zz, T), :] = (total * (1.0 - c * c)).astype(BF16)
+
+    def hid_part(s):
+        total = jnp.zeros((T, E), F32)
+        for k in range(K):
+            total = total + lax.dot_general(
+                pg[k, rows_of(z, T), :], w[k, rows_of(s, E), :], NT,
+                preferred_element_type=F32)
+        return total
+
+    @scoped
+    def hid_send(d):
+        s = lax.rem(me_v + d, N)
+        if d == 0:
+            own_hs[...] = hid_part(s)
+        else:
+            hss[d] = hid_part(s).astype(BF16)
+            send(hss.at[d], hsr.at[d], hs_s.at[d], hs_r.at[d], {"voc": s})
+
+    @scoped
+    def pair_sums():
+        for zz in range(Z):
+            arrived(vgy.at[zz], vy_r.at[zz], vy_s.at[zz])
+            vsum[zz] = vgb[rows_of(zz * 2 + y, R), :].astype(F32) + vgy[zz].astype(F32)
+
+    @scoped
+    def hop(h):
+        for way, at, ends in ((0, h, range(h + 1, Z)), (1, Z - 1 - h, range(Z - 1 - h))):
+            copies = [
+                remote(vout.at[way, e], vin.at[way, e], vz_s.at[way, e], vz_r.at[way, e],
+                       {"tok": me_t + 2 - 4 * way})
+                for e in ends
+            ]
+
+            @pl.when(z == at)
+            def _(way=way, ends=ends, copies=copies):
+                for e, c in zip(ends, copies):
+                    part = vsum[e]
+                    if h > 0:
+                        arrived(vin.at[way, e], vz_r.at[way, e], vz_s.at[way, e])
+                        part = part + vin[way, e].astype(F32)
+                    vout[way, e] = part.astype(BF16)
+                    c.start()
+            for c in copies:
+                sends.append((z == at, c))
+
+    pieces = [(k, 0, E) for k in range(K)]
+    if E % 256 == 0:
+        pieces[-1:] = [(K - 1, 0, E // 2), (K - 1, E // 2, E // 2)]
+
+    @scoped
+    def proj_part(k):
+        for p, (kk, lo, wide) in enumerate(pieces):
+            if kk == k:
+                lanes = slice(lo, lo + wide)
+                psend[k, :, lanes] = jnp.dot(
+                    htr[1 - y], pg[k, :, lanes], preferred_element_type=F32).astype(BF16)
+                send(psend.at[k, :, pl.ds(lo, wide)], precv.at[k, :, pl.ds(lo, wide)],
+                     pp_s.at[p], pp_r.at[p], {"tok": ypart})
+        acc[k] = jnp.dot(htr[y], pg[k], preferred_element_type=F32)
+
+    @scoped
+    def vocab_part():
+        for s in range(N):
+            total = None
+            for k in range(K):
+                part = lax.dot_general(ctx[s, k * T:(k + 1) * T, :], lgall[z, me_v, k], TN,
+                                       preferred_element_type=F32)
+                total = part if total is None else total + part
+            vgb[s * E:(s + 1) * E, :] = total.astype(BF16)
+        for zz in range(Z):
+            send(vgb.at[pl.ds((zz * 2 + 1 - y) * R, R)], vgy.at[zz], vy_s.at[zz], vy_r.at[zz],
+                 {"tok": ypart})
+
+    @scoped
+    def vw_done():
+        vwe[me_v] = vw[rows_of(me_v, E), :]
+        arrived(vwe.at[partner], vp_r.at[0], vp_s.at[0])
+        for i in range(1, half):
+            ci = lax.rem(chip + i, half)
+            for zz in range(Z):
+                t = zz * 2 + 1 - y
+                arrived(vw_piece(ci, t), vw_r.at[ci, t], vwy_s.at[i, zz])
+        for s in range(N):
+            vwt[s] = vwe[s].T
+
+    @scoped
+    def turn():
+        for b in range(2):
+            col = (z * 2 + b) * R
+            for zz in range(Z):
+                htr[b, :, zz * T:(zz + 1) * T] = hida[
+                    zz, col // H, :, pl.ds(pl.multiple_of(col % H, R), R)].T
+
+    lag = 2
+    hid_order = list(range(1, N)) + [0]
+    for step in range(K + Z + lag):
+        if step < K:
+            own_out(step)
+        if step == 1:
+            vocab_part()
+        for j in range(1, Z):
+            if 0 <= step - (j + 1) // 2 < K:
+                relay_lg(step - (j + 1) // 2, j, True)
+        for j in range(1, Z):
+            if 0 <= step - j < K:
+                relay_lg(step - j, j, False)
+        if step == 3:
+            for j in range(3, Z):
+                relay_hid(j, False)
+        for j in range(Z):
+            if 0 <= step - j - 1 < K:
+                cross_lg(step - j - 1, j)
+        for j in range(Z):
+            k = step - lag - j
+            if not 0 <= k < K:
+                continue
+            if k == 0 and j > 1:
+                ctx_mate(j, range(K))
+            if k == 0 and j == 0:
+                vw_done()
+            pre_grad(k, j)
+            if k == 0 and j == Z - 1:
+                turn()
+            if j == Z - 1:
+                proj_part(k)
+                for d in hid_order[k * N // K:(k + 1) * N // K]:
+                    hid_send(d)
+        if step == K:
+            pair_sums()
+        if K <= step < K + Z - 1:
+            hop(step - K)
+
+    acc_v = vsum.at[z]
+    for way, pred in ((0, has_l), (1, has_r)):
+        @pl.when(pred)
+        def _(way=way):
+            arrived(vin.at[way, z], vz_r.at[way, z], vz_s.at[way, z])
+            acc_v[...] += vin[way, z].astype(F32)
+    out_vocab[...] = acc_v[...].astype(BF16)
+    htot = own_hs[...]
+    for d in range(1, N):
+        arrived(hsr.at[d], hs_r.at[d], hs_s.at[d])
+        htot = htot + hsr[d].astype(F32)
+    mixf = mix[...].astype(F32)
+    for k in range(K):
+        htot = htot + column(mgrad[k:k + 1, :], E) * mixf[k:k + 1, :]
+    out_hidden[...] = htot.astype(BF16)
+
+    back = mix_rows(K, True)
+    for p, (k, lo, wide) in enumerate(pieces):
+        lanes = slice(lo, lo + wide)
+        with jax.named_scope("precv"):
+            arrived(precv.at[k, :, pl.ds(lo, wide)], pp_r.at[p], pp_s.at[p])
+        psum = (acc[k, :, lanes] + precv[k, :, lanes].astype(F32)).astype(BF16)
+        if k < K - 1:
+            precv[k, :, lanes] = psum
+            continue
+        for b in range(R // B):
+            rows = slice(b * B, (b + 1) * B)
+            x = jnp.concatenate([precv[q, rows, lanes] for q in range(K - 1)] + [psum[rows]], axis=0)
+            out = jnp.dot(back, x, preferred_element_type=F32).astype(BF16)
+            for j in range(wide // 128):
+                out_proj.at[lo // 128 + j].reshape(R * K, 128)[b * 256:(b + 1) * 256, :] = (
+                    out[:, j * 128:(j + 1) * 128])
+    with jax.named_scope("drain"):
+        for pred, c in sends:
+            if pred is None:
+                c.wait_send()
+            else:
+                pl.when(pred)(c.wait_send)
+
+
+def body_fast(M, N, hidden, mix_weight, comp_proj, vocab_weight, log_normalizer, targets, loss_grad):
+    T, D = hidden.shape
+    K, E = mix_weight.shape
+    V = vocab_weight.shape[1]
+    R = D // M
+    J = E // 128
+    half = N // 2
+    Z = M // 2
+    vm = pltpu.VMEM
+    dma = pltpu.SemaphoreType.DMA
+    scratch = [
+        vm((J, D, K, 128), BF16), vm((K, D, E), BF16), vm((Z, 2, T, D // 2), BF16), vm((D, V), BF16),
+        vm((N, E, V), BF16), vm((N, V, E), BF16), vm((K, E), BF16), vm((K, T), F32), vm((1, T), jnp.int32), vm((1, T), F32),
+        vm((N, K * T, E), BF16), vm((Z, K * T, E), BF16), vm((N, K, E), BF16), vm((2, R, Z * T), BF16),
+        vm((K * T, V), F32), vm((Z, N, K, T, V), BF16), vm((N, 8, T), F32), vm((K, Z * T, E), BF16),
+        vm((D, V), BF16), vm((Z, R, V), BF16),
+        vm((Z, R, V), F32), vm((2, Z, R, V), BF16), vm((2, Z, R, V), BF16),
+        vm((N, T, E), BF16), vm((N, T, E), BF16),
+        vm((T, E), F32), vm((K, R, E), F32), vm((K, R, E), BF16), vm((K, R, E), BF16),
+        vm((K, T), F32),
+        dma((7,)), dma((4, J)),
+        dma((half, K)), dma((half, K)), dma((N, K)), dma((N,)), dma((N,)),
+        dma((2, Z)), dma((Z,)), dma((Z,)), dma((Z,)),
+        dma((half, 2)), dma((N,)), dma((1,)), dma((1,)),
+        dma((half, Z)), dma((half, Z)), dma((half, M)), dma((N,)), dma((N,)),
+        dma((2, Z, K)), dma((half, Z, K)), dma((half, Z, K)), dma((Z, N, K)),
+        dma((Z,)), dma((Z,)), dma((2, Z)), dma((2, Z)), dma((N,)), dma((N,)),
+        dma((K + 1,)), dma((K + 1,)),
+    ]
+    spec = pl.BlockSpec(memory_space=pltpu.VMEM)
+    hbm = pl.BlockSpec(memory_space=pltpu.MemorySpace.HBM)
+    hid, proj, voc = pl.pallas_call(
+        functools.partial(fast_kernel, M, N),
+        out_shape=(
+            jax.ShapeDtypeStruct((T, E), BF16),
+            jax.ShapeDtypeStruct((J, R, K, 128), BF16),
+            jax.ShapeDtypeStruct((R, V), BF16),
+        ),
+        in_specs=[hbm] * 7,
+        out_specs=(spec, spec, spec),
+        scratch_shapes=scratch,
+        compiler_params=pltpu.CompilerParams(
+            collective_id=0, has_side_effects=True, vmem_limit_bytes=47 * 1024 * 1024
+        ),
+    )(*[
+        pltpu.with_memory_space_constraint(x, pltpu.MemorySpace.HBM)
+        for x in (hidden, mix_weight, comp_proj, vocab_weight, log_normalizer, targets[None, :], loss_grad[None, :])
+    ])
+    return pl.pallas_call(
+        store_kernel,
+        out_shape=(
+            jax.ShapeDtypeStruct((T, E), BF16),
+            jax.ShapeDtypeStruct((R, K, E), BF16),
+            jax.ShapeDtypeStruct((R, V), BF16),
+        ),
+        in_specs=[spec] * 3,
+        out_specs=(hbm, hbm, hbm),
+        scratch_shapes=[dma((J + 2,))],
+        compiler_params=pltpu.CompilerParams(vmem_limit_bytes=4 * 1024 * 1024),
+    )(hid, proj, voc)
+
+
+def store_kernel(hid, proj, voc, out_hid, out_proj, out_voc, sem):
+    J = proj.shape[0]
+    copies = [pltpu.make_async_copy(hid, out_hid, sem.at[J]), pltpu.make_async_copy(voc, out_voc, sem.at[J + 1])]
+    for j in range(J):
+        copies.append(pltpu.make_async_copy(proj.at[j], out_proj.at[:, :, pl.ds(j * 128, 128)], sem.at[j]))
+    for c in copies:
+        c.start()
+    for c in copies:
+        c.wait()
+
+
+def body(M, N, *args):
+    hidden, mix_weight, comp_proj, vocab_weight = args[:4]
+    T, D = hidden.shape
+    K, E = mix_weight.shape
+    V = vocab_weight.shape[1]
+    gathered = 2 * (M // 2) * T * (K * N * V + D + 2 * K * E)
+    shapes = K == 4 and E % 128 == 0 and (E // M) % 16 == 0 and (D // M) % (256 // K) == 0
+    if shapes and gathered + 4 * K * D * E <= 28 * 1024 * 1024:
+        return body_fast(M, N, *args)
+    return body_base(M, N, *args)
+
+
 def solution(mesh):
     in_specs = (
         P("tok", None),

time: 92.6 us -> 82.9 us (0.90)
  local copies, waits for them, and re-layouts: 11.5 us -> 0 us
  Pallas kernels: 80.2 us -> 81.9 us
    unnamed x16 -> x0, local copies, waits for them, and re-layouts: 11.5 us -> none
    pallas_call x1 -> x2, Pallas kernels: 80.2 us -> 81.9 us  [the longest x1 80.8 us: body_fast(): pl.pallas_call(functools.partial(fast_kernel, M, N), out_shape=(jax.Shape...]
where the time goes in v1:
time: 82.9 us; the launch traced here: 82.7 us
  Pallas kernels  81.9 us (99%)
    pallas_call x1, Pallas kernels, body_fast(): pl.pallas_call(functools.partial(fast_kernel, M, N), out_shape=(jax.Shape...  80.8 us

profile of v1, /device:TPU:0, one launch (start us, length us, event | category | flops | bytes accessed | tf_op | source)
XLA Modules:
  0.0 82.7 jit_solution(11751011725343367128)
XLA Ops:
  0.6 80.8 %shard_map.94 = (bf16[128,512]{1,0:T(8,128)(2,1)S(1)}, bf16[4,256,4,128]{3,2,1,0:T(4,128)(2,1)S(1)}, bf16[256,256]{1,0:T(8,128)(2,1)S(1)}) custom-call(bf16[128,2048]{1,0:T(8,128)(2,1)} %hid_hbm.1, bf16[4,512]{1,0:T(4,128)(2,1)} %mix_hbm.1, bf16[2048,4,512]{2,1,0:T(4,128)(2,1)} %proj_hbm.1, bf16[2048,256]{1,0:T(8,128)(2,1)} %vw_hbm.1, f32[4,128]{1,0:T(4,128)} %logz_hbm.1, ...), custom_call_target="tpu_custom_call" | custom-call | tf_op jit(solution)/shard_map/pallas_call | solution.py:925
  81.5 1.1 %shard_map.95 = (bf16[128,512]{1,0:T(8,128)(2,1)}, bf16[256,4,512]{2,1,0:T(4,128)(2,1)}, bf16[256,256]{1,0:T(8,128)(2,1)}) custom-call(bf16[128,512]{1,0:T(8,128)(2,1)S(1)} %get-tuple-element.6.hid, bf16[4,256,4,128]{3,2,1,0:T(4,128)(2,1)S(1)} %get-tuple-element.7.proj, bf16[256,256]{1,0:T(8,128)(2,1)S(1)} %get-tuple-element.8.voc), custom_call_target="tpu_custom_call" | custom-call | tf_op jit(solution)/shard_map/pallas_call | solution.py:942

commit v2 on v1

--- a/solution.py
+++ b/solution.py
@@ -381,11 +381,11 @@
     hid_hbm, mix_hbm, proj_hbm, vw_hbm, logz_hbm, tg_hbm, loss_hbm,
     out_hidden, out_proj, out_vocab,
     raw, w, hida, vw, vwe, vwt, mix, logz, targets, loss,
-    ctx, ctxz, mix_all, htr, logit, lgall, tgt, pg,
+    ctx, ctxz, mix_all, htr, logit, lg, lgall, tgt, scale, pg,
     vgb, vgy, vsum, vout, vin, hss, hsr, own_hs, acc, psend, precv, mgrad,
     l_sem, w_sem, ctx_s, ctx_f, ctx_r, mix_s, mix_r, hz_s, hz_r, hp_s, hp_r,
     vx_s, vx_r, vp_s, vp_r, vwz_s, vwy_s, vw_r, tgt_s, tgt_r,
-    lz_s, lx_s, lp_s, lg_r, vy_s, vy_r, vz_s, vz_r, hs_s, hs_r, pp_s, pp_r,
+    lz_s, lx_s, lp_s, lg_r, vy_s, vy_r, vz_s, vz_r, hs_s, hs_r, pp_s, pp_r, sc_s, sc_r,
 ):
     K, D, E = w.shape
     T = hida.shape[2]
@@ -501,6 +501,9 @@
             for d in range(1, Z):
                 send(piece, piece, vwz_s.at[i, d], vw_r.at[ci, me_t], {"tok": lax.rem(me_t + 2 * d, M)})
 
+    def hid_piece(zz, side, p):
+        return hida.at[zz, side, pl.ds(p * (T // 2), T // 2)]
+
     def slab(v, t):
         return pl.ds(pl.multiple_of(v * E + t * S, S), S)
 
@@ -509,8 +512,10 @@
             v = lax.rem(chip + i, half) * 2 + c
             send(vw.at[slab(v, me_t)], vwe.at[me_v, rows_of(me_t, S)],
                  vx_s.at[i, c], vx_r.at[me_v], {"voc": v})
-    send(hida.at[z, core], hida.at[z, core], hz_s.at[0, z], hz_r.at[z], {"tok": me_t + 2}, has_r)
-    send(hida.at[z, core], hida.at[z, core], hz_s.at[1, z], hz_r.at[z], {"tok": me_t - 2}, has_l)
+    for p in range(2):
+        piece = hid_piece(z, core, p)
+        send(piece, piece, hz_s.at[0, z, p], hz_r.at[z, p], {"tok": me_t + 2}, has_r)
+        send(piece, piece, hz_s.at[1, z, p], hz_r.at[z, p], {"tok": me_t - 2}, has_l)
     for c in loads[3:]:
         c.wait()
     for d in range(1, N):
@@ -550,16 +555,16 @@
             send(piece, piece, vwy_s.at[i, zz], vw_r.at[ci, t], {"tok": ypart})
 
     @scoped
-    def relay_hid(j, fwd):
+    def relay_hid(j, p, fwd):
         zz = mate(j)
         there, to = onward(zz)
-        piece = hida.at[zz, core]
-        on = remote(piece, piece, hz_s.at[0, zz], hz_r.at[zz], {"tok": to})
-        over = remote(piece, piece, hp_s.at[zz], hp_r.at[zz], {"voc": partner})
+        piece = hid_piece(zz, core, p)
+        on = remote(piece, piece, hz_s.at[0, zz, p], hz_r.at[zz, p], {"tok": to})
+        over = remote(piece, piece, hp_s.at[zz, p], hp_r.at[zz, p], {"voc": partner})
 
         @pl.when(there if fwd else jnp.logical_not(there))
         def _():
-            arrived(piece, hz_r.at[zz], hz_s.at[0, zz])
+            arrived(piece, hz_r.at[zz, p], hz_s.at[0, zz, p])
             if fwd:
                 on.start()
             over.start()
@@ -571,7 +576,8 @@
     def ctx_mate(j, ks):
         zz = mate(j)
         if ks[0] == 0:
-            arrived(hida.at[zz, 1 - core], hp_r.at[zz], hp_s.at[zz])
+            for p in range(2):
+                arrived(hid_piece(zz, 1 - core, p), hp_r.at[zz, p], hp_s.at[zz, p])
         for k in ks:
             ctxz[zz, k * T:(k + 1) * T, :] = context(zz, k)
 
@@ -584,6 +590,8 @@
             send(piece, piece, ctx_f.at[i, k], ctx_r.at[s, k], {"voc": partner})
 
     add_logits(me_v, True)
+    for j in range(1, min(Z, 3)):
+        relay_hid(j, 0, True)
     for k in range(K):
         arrived(ctx.at[partner, pl.ds(k * T, T)], ctx_r.at[partner, k], ctx_s.at[0, k])
     add_logits(partner)
@@ -604,18 +612,26 @@
     exp_mix = jnp.exp(mixing)
     weights = exp_mix / jnp.sum(exp_mix, axis=0, keepdims=True)
 
+    for j in range(1, min(Z, 3)):
+        relay_hid(j, 1, True)
     ctx_pass(0)
-    for j in range(1, min(Z, 3)):
-        relay_hid(j, True)
     if Z > 1:
-        relay_hid(1, False)
+        relay_hid(1, 0, False)
+        relay_hid(1, 1, False)
     ctx_pass(1)
     for j in range(1, Z):
         relay_vw(j)
     if Z > 1:
         ctx_mate(1, range(K))
-    for k in range(2, K):
+    ctx_pass(2)
+    for j in range(3, Z):
+        relay_hid(j, 0, True)
+    if Z > 2:
+        relay_hid(2, 0, False)
+    for k in range(3, K):
         ctx_pass(k)
+    if Z > 2:
+        relay_hid(2, 1, False)
     for i in range(1, half):
         add_logits(lax.rem(chip - i + half, half) * 2 + core)
     for i in range(1, half):
@@ -632,24 +648,20 @@
     tgt[0] = table.T[0:8, :]
     for d in range(1, N):
         send(tgt.at[0], tgt.at[d], tgt_s.at[d], tgt_r.at[d], {"voc": lax.rem(me_v + d, N)})
-    for j in range(3, Z):
-        relay_hid(j, True)
-    if Z > 2:
-        relay_hid(2, False)
-    for k in range(K):
-        rows = slice(k * T, (k + 1) * T)
-        logit[rows, :] = jnp.exp(logit[rows, :] - column(logz[k:k + 1, :], V)) - onehot
-    with jax.named_scope("targets"):
+    @scoped
+    def scales():
         for d in range(1, N):
             arrived(tgt.at[d], tgt_r.at[d], tgt_s.at[d])
-    target = tgt[0]
-    for d in range(1, N):
-        target = target + tgt[d]
-    likely = jnp.exp(target[0:K, :] - logz[...])
-    joint = weights * likely
-    posterior = joint / jnp.sum(joint, axis=0, keepdims=True)
-    factor = loss[...] * posterior
-    mgrad[...] = loss[...] * (weights - posterior)
+        target = tgt[0]
+        for d in range(1, N):
+            target = target + tgt[d]
+        likely = jnp.exp(target[0:K, :] - logz[...])
+        joint = weights * likely
+        posterior = joint / jnp.sum(joint, axis=0, keepdims=True)
+        scale[z, 0:K, :] = loss[...] * posterior
+        mgrad[...] = loss[...] * (weights - posterior)
+        for d in range(1, Z):
+            send(scale.at[z], scale.at[z], sc_s.at[d], sc_r.at[z], {"tok": lax.rem(me_t + 2 * d, M)})
 
     def shares(zz, k):
         piece = lgall.at[zz, me_v, k]
@@ -664,19 +676,18 @@
             c.start()
             sends.append((None, c))
 
-    def fill(ks):
-        for k in ks:
-            rows = slice(k * T, (k + 1) * T)
-            lgall[z, me_v, k] = (column(factor[k:k + 1, :], V) * logit[rows, :]).astype(BF16)
-
     @scoped
     def own_out(k):
-        if k < 2:
-            fill(range(K)[k:] if k else range(1))
+        rows = slice(k * T, (k + 1) * T)
+        logit[rows, :] = jnp.exp(logit[rows, :] - column(logz[k:k + 1, :], V)) - onehot
+        lgall[z, me_v, k] = logit[rows, :].astype(BF16)
+        share(z, k)
+
+    @scoped
+    def own_line(k):
         piece = lgall.at[z, me_v, k]
         send(piece, piece, lz_s.at[0, z, k], lg_r.at[z, me_v, k], {"tok": me_t + 2}, has_r)
         send(piece, piece, lz_s.at[1, z, k], lg_r.at[z, me_v, k], {"tok": me_t - 2}, has_l)
-        share(z, k)
 
     @scoped
     def relay_lg(k, j, fwd):
@@ -718,6 +729,10 @@
             part = jnp.dot(lgall[zz, s, k], vwt[s], preferred_element_type=F32)
             total = part if total is None else total + part
         c = (ctx[me_v, rows, :] if j == 0 else ctxz[zz, rows, :]).astype(F32)
+        if k == 0:
+            if j > 0:
+                arrived(scale.at[zz], sc_r.at[zz], sc_s.at[1])
+        total = total * column(scale[zz, k:k + 1, :], E)
         pg[k, rows_of(zz, T), :] = (total * (1.0 - c * c)).astype(BF16)
 
     def hid_part(s):
@@ -739,30 +754,15 @@
 
     @scoped
     def pair_sums():
-        for zz in range(Z):
+        for d in list(range(1, Z)) + [0]:
+            zz = lax.rem(z + d, Z)
             arrived(vgy.at[zz], vy_r.at[zz], vy_s.at[zz])
-            vsum[zz] = vgb[rows_of(zz * 2 + y, R), :].astype(F32) + vgy[zz].astype(F32)
-
-    @scoped
-    def hop(h):
-        for way, at, ends in ((0, h, range(h + 1, Z)), (1, Z - 1 - h, range(Z - 1 - h))):
-            copies = [
-                remote(vout.at[way, e], vin.at[way, e], vz_s.at[way, e], vz_r.at[way, e],
-                       {"tok": me_t + 2 - 4 * way})
-                for e in ends
-            ]
-
-            @pl.when(z == at)
-            def _(way=way, ends=ends, copies=copies):
-                for e, c in zip(ends, copies):
-                    part = vsum[e]
-                    if h > 0:
-                        arrived(vin.at[way, e], vz_r.at[way, e], vz_s.at[way, e])
-                        part = part + vin[way, e].astype(F32)
-                    vout[way, e] = part.astype(BF16)
-                    c.start()
-            for c in copies:
-                sends.append((z == at, c))
+            total = vgb[rows_of(zz * 2 + y, R), :].astype(F32) + vgy[zz].astype(F32)
+            if d == 0:
+                vsum[...] = total
+            else:
+                vout[zz] = total.astype(BF16)
+                send(vout.at[zz], vin.at[z], vz_s.at[d], vz_r.at[z], {"tok": zz * 2 + y})
 
     pieces = [(k, 0, E) for k in range(K)]
     if E % 256 == 0:
@@ -781,13 +781,12 @@
 
     @scoped
     def vocab_part():
+        for k in range(K):
+            rows = slice(k * T, (k + 1) * T)
+            lg[rows, :] = (column(scale[z, k:k + 1, :], V) * logit[rows, :]).astype(BF16)
         for s in range(N):
-            total = None
-            for k in range(K):
-                part = lax.dot_general(ctx[s, k * T:(k + 1) * T, :], lgall[z, me_v, k], TN,
-                                       preferred_element_type=F32)
-                total = part if total is None else total + part
-            vgb[s * E:(s + 1) * E, :] = total.astype(BF16)
+            vgb[s * E:(s + 1) * E, :] = lax.dot_general(
+                ctx[s], lg[...], TN, preferred_element_type=F32).astype(BF16)
         for zz in range(Z):
             send(vgb.at[pl.ds((zz * 2 + 1 - y) * R, R)], vgy.at[zz], vy_s.at[zz], vy_r.at[zz],
                  {"tok": ypart})
@@ -812,52 +811,49 @@
                 htr[b, :, zz * T:(zz + 1) * T] = hida[
                     zz, col // H, :, pl.ds(pl.multiple_of(col % H, R), R)].T
 
-    lag = 2
     hid_order = list(range(1, N)) + [0]
-    for step in range(K + Z + lag):
-        if step < K:
-            own_out(step)
-        if step == 1:
-            vocab_part()
+    events = []
+
+    def at(time, fn, *args):
+        events.append((time, len(events), fn, args))
+
+    late = [1.2 + 2.2 * (k - 1) if k else 0.0 for k in range(K)]
+    for k in range(K):
+        at(0.01 * k, own_out, k)
+        at(0.01 * k if k < 2 else 3.0 + 1.62 * (k - 2), own_line, k)
         for j in range(1, Z):
-            if 0 <= step - (j + 1) // 2 < K:
-                relay_lg(step - (j + 1) // 2, j, True)
+            at(late[k] + 2.2 * ((j + 1) // 2), relay_lg, k, j, True)
         for j in range(1, Z):
-            if 0 <= step - j < K:
-                relay_lg(step - j, j, False)
-        if step == 3:
-            for j in range(3, Z):
-                relay_hid(j, False)
+            at(late[k] + 2.2 * j, relay_lg, k, j, False)
         for j in range(Z):
-            if 0 <= step - j - 1 < K:
-                cross_lg(step - j - 1, j)
-        for j in range(Z):
-            k = step - lag - j
-            if not 0 <= k < K:
-                continue
-            if k == 0 and j > 1:
-                ctx_mate(j, range(K))
-            if k == 0 and j == 0:
-                vw_done()
-            pre_grad(k, j)
-            if k == 0 and j == Z - 1:
-                turn()
-            if j == Z - 1:
-                proj_part(k)
-                for d in hid_order[k * N // K:(k + 1) * N // K]:
-                    hid_send(d)
-        if step == K:
-            pair_sums()
-        if K <= step < K + Z - 1:
-            hop(step - K)
-
-    acc_v = vsum.at[z]
-    for way, pred in ((0, has_l), (1, has_r)):
-        @pl.when(pred)
-        def _(way=way):
-            arrived(vin.at[way, z], vz_r.at[way, z], vz_s.at[way, z])
-            acc_v[...] += vin[way, z].astype(F32)
-    out_vocab[...] = acc_v[...].astype(BF16)
+            time = 2.2 * (j + 1) + (1.2 * k if j == 0 else 1.2 * late[k])
+            at(time, cross_lg, k, j)
+            at(time + (0.8 if j == Z - 1 else 1.2), pre_grad, k, j)
+        at(2.2 * Z + 1.2 * late[k] + 0.81, proj_part, k)
+        if k > 0:
+            for d in hid_order[(k - 1) * N // K:(k if k < K - 1 else K) * N // K]:
+                at(2.2 * Z + 1.2 * late[k] + 0.82, hid_send, d)
+    at(2.201, scales)
+    if Z > 2:
+        at(0.3, ctx_mate, 2, range(K))
+    at(2.202, vocab_part)
+    for j in range(3, Z):
+        at(0.2, relay_hid, j, 1, True)
+        at(2.25, relay_hid, j, 0, False)
+        at(3.35, relay_hid, j, 1, False)
+        at(4.5, ctx_mate, j, range(K))
+    at(2.21, vw_done)
+    at(4.6, turn)
+    at(13.5, pair_sums)
+    for _, _, fn, args in sorted(events, key=lambda e: e[:2]):
+        fn(*args)
+
+    vtot = vsum[...]
+    for d in range(1, Z):
+        zz = lax.rem(z + d, Z)
+        arrived(vin.at[zz], vz_r.at[zz], vz_s.at[d])
+        vtot = vtot + vin[zz].astype(F32)
+    out_vocab[...] = vtot.astype(BF16)
     htot = own_hs[...]
     for d in range(1, N):
         arrived(hsr.at[d], hs_r.at[d], hs_s.at[d])
@@ -905,20 +901,20 @@
         vm((J, D, K, 128), BF16), vm((K, D, E), BF16), vm((Z, 2, T, D // 2), BF16), vm((D, V), BF16),
         vm((N, E, V), BF16), vm((N, V, E), BF16), vm((K, E), BF16), vm((K, T), F32), vm((1, T), jnp.int32), vm((1, T), F32),
         vm((N, K * T, E), BF16), vm((Z, K * T, E), BF16), vm((N, K, E), BF16), vm((2, R, Z * T), BF16),
-        vm((K * T, V), F32), vm((Z, N, K, T, V), BF16), vm((N, 8, T), F32), vm((K, Z * T, E), BF16),
+        vm((K * T, V), F32), vm((K * T, V), BF16), vm((Z, N, K, T, V), BF16), vm((N, 8, T), F32), vm((Z, 8, T), F32), vm((K, Z * T, E), BF16),
         vm((D, V), BF16), vm((Z, R, V), BF16),
-        vm((Z, R, V), F32), vm((2, Z, R, V), BF16), vm((2, Z, R, V), BF16),
+        vm((R, V), F32), vm((Z, R, V), BF16), vm((Z, R, V), BF16),
         vm((N, T, E), BF16), vm((N, T, E), BF16),
         vm((T, E), F32), vm((K, R, E), F32), vm((K, R, E), BF16), vm((K, R, E), BF16),
         vm((K, T), F32),
         dma((7,)), dma((4, J)),
         dma((half, K)), dma((half, K)), dma((N, K)), dma((N,)), dma((N,)),
-        dma((2, Z)), dma((Z,)), dma((Z,)), dma((Z,)),
+        dma((2, Z, 2)), dma((Z, 2)), dma((Z, 2)), dma((Z, 2)),
         dma((half, 2)), dma((N,)), dma((1,)), dma((1,)),
         dma((half, Z)), dma((half, Z)), dma((half, M)), dma((N,)), dma((N,)),
         dma((2, Z, K)), dma((half, Z, K)), dma((half, Z, K)), dma((Z, N, K)),
-        dma((Z,)), dma((Z,)), dma((2, Z)), dma((2, Z)), dma((N,)), dma((N,)),
-        dma((K + 1,)), dma((K + 1,)),
+        dma((Z,)), dma((Z,)), dma((Z,)), dma((Z,)), dma((N,)), dma((N,)),
+        dma((K + 1,)), dma((K + 1,)), dma((Z,)), dma((Z,)),
     ]
     spec = pl.BlockSpec(memory_space=pltpu.VMEM)
     hbm = pl.BlockSpec(memory_space=pltpu.MemorySpace.HBM)

time: 82.9 us -> 74.3 us (0.90)
  Pallas kernels: 81.9 us -> 73.3 us
    pallas_call x1, Pallas kernels: 80.8 us -> 72.2 us  [body_fast(): pl.pallas_call(functools.partial(fast_kernel, M, N), out_shape=(jax.Shape...]
where the time goes in v2:
time: 74.3 us; the launch traced here: 74.1 us
  Pallas kernels  73.3 us (99%)
  between operations  0.8 us (1%)
    pallas_call x1, Pallas kernels, body_fast(): pl.pallas_call(functools.partial(fast_kernel, M, N), out_shape=(jax.Shape...  72.2 us

profile of v2, /device:TPU:0, one launch (start us, length us, event | category | flops | bytes accessed | tf_op | source)
XLA Modules:
  0.0 74.1 jit_solution(12861434412760164354)
XLA Ops:
  0.6 72.2 %shard_map.94 = (bf16[128,512]{1,0:T(8,128)(2,1)S(1)}, bf16[4,256,4,128]{3,2,1,0:T(4,128)(2,1)S(1)}, bf16[256,256]{1,0:T(8,128)(2,1)S(1)}) custom-call(bf16[128,2048]{1,0:T(8,128)(2,1)} %hid_hbm.1, bf16[4,512]{1,0:T(4,128)(2,1)} %mix_hbm.1, bf16[2048,4,512]{2,1,0:T(4,128)(2,1)} %proj_hbm.1, bf16[2048,256]{1,0:T(8,128)(2,1)} %vw_hbm.1, f32[4,128]{1,0:T(4,128)} %logz_hbm.1, ...), custom_call_target="tpu_custom_call" | custom-call | tf_op jit(solution)/shard_map/pallas_call | solution.py:921
  72.8 1.1 %shard_map.95 = (bf16[128,512]{1,0:T(8,128)(2,1)}, bf16[256,4,512]{2,1,0:T(4,128)(2,1)}, bf16[256,256]{1,0:T(8,128)(2,1)}) custom-call(bf16[128,512]{1,0:T(8,128)(2,1)S(1)} %get-tuple-element.6.hid, bf16[4,256,4,128]{3,2,1,0:T(4,128)(2,1)S(1)} %get-tuple-element.7.proj, bf16[256,256]{1,0:T(8,128)(2,1)S(1)} %get-tuple-element.8.voc), custom_call_target="tpu_custom_call" | custom-call | tf_op jit(solution)/shard_map/pallas_call | solution.py:938

commit v3 on v2

--- a/solution.py
+++ b/solution.py
@@ -361,6 +361,19 @@
     return hidden_grad, jnp.transpose(proj_grad, (1, 0, 2)), vocab_grad
 
 
+ORDER = (
+    (0, 0), (0, 2), (2, 0), (11, 3, 0), (0, 1), (2, 1), (1, 1), (1, 2), (10, 2), (0, 3), (1, 0), (8,),
+    (3, 0, 2), (3, 0, 1), (9,), (3, 0, 3), (4, 0, 1), (3, 1, 1), (4, 1, 1), (11, 3, 1), (4, 0, 2),
+    (3, 1, 2), (2, 2), (12,), (4, 0, 3), (10, 3), (4, 1, 2), (5, 0, 2), (1, 3), (5, 0, 1), (5, 0, 0),
+    (13,), (3, 1, 3), (2, 3), (6, 0, 2), (5, 0, 3), (5, 1, 0), (6, 0, 1), (6, 0, 0), (3, 2, 1), (3, 2, 2),
+    (4, 1, 3), (4, 2, 1), (5, 1, 1), (6, 0, 3), (7, 0), (4, 2, 2), (5, 2, 0), (3, 2, 3), (5, 1, 2),
+    (3, 3, 2), (3, 3, 1), (6, 1, 0), (5, 3, 0), (4, 2, 3), (5, 1, 3), (6, 1, 1), (4, 3, 2), (6, 1, 2),
+    (6, 1, 3), (7, 1), (3, 3, 3), (4, 3, 1), (5, 2, 3), (4, 3, 3), (5, 2, 1), (5, 2, 2), (6, 3, 0),
+    (6, 2, 2), (6, 2, 0), (5, 3, 1), (6, 2, 3), (15,), (5, 3, 2), (6, 2, 1), (7, 2), (5, 3, 3), (6, 3, 1),
+    (14, 1), (6, 3, 2), (6, 3, 3), (7, 3), (14, 0), (14, 2), (14, 3),
+)
+
+
 def scoped(fn):
     def run(*args, **kw):
         tag = "_".join(str(a) for a in args if isinstance(a, int))
@@ -384,7 +397,7 @@
     ctx, ctxz, mix_all, htr, logit, lg, lgall, tgt, scale, pg,
     vgb, vgy, vsum, vout, vin, hss, hsr, own_hs, acc, psend, precv, mgrad,
     l_sem, w_sem, ctx_s, ctx_f, ctx_r, mix_s, mix_r, hz_s, hz_r, hp_s, hp_r,
-    vx_s, vx_r, vp_s, vp_r, vwz_s, vwy_s, vw_r, tgt_s, tgt_r,
+    vx_s, vx_r, vp_s, vp_r, vwz_s, vwz_r, vwy_s, vwy_r, tgt_s, tgt_r,
     lz_s, lx_s, lp_s, lg_r, vy_s, vy_r, vz_s, vz_r, hs_s, hs_r, pp_s, pp_r, sc_s, sc_r,
 ):
     K, D, E = w.shape
@@ -393,7 +406,6 @@
     V = vw.shape[1]
     R = D // M
     J = E // 128
-    S = E // M
     half = N // 2
     Z = M // 2
     B = 256 // K
@@ -487,31 +499,42 @@
     with jax.named_scope("barrier"):
         pl.semaphore_wait(bar, M + N - 2)
 
-    def vw_piece(ci, t):
-        return vwe.at[pl.ds(ci * 2, 2), rows_of(t, S)]
-
-    @scoped
-    def vw_own():
+    g = z % 2
+    zpair = me_t + 2 - 4 * g
+
+    def vw_rows(yy, part):
+        return pl.ds(pl.multiple_of(yy * (E // 2) + part * (E // 4), E // 4), E // 4)
+
+    def vw_send():
+        for i in range(1, half):
+            for c in range(2):
+                v = lax.rem(chip + i, half) * 2 + c
+                rows = vw_rows(y, g)
+                send(vw.at[pl.ds(pl.multiple_of(v * E + rows.start, E // 4), rows.size)],
+                     vwe.at[me_v, rows], vx_s.at[i, c], vx_r.at[me_v], {"voc": v})
+
+    @scoped
+    def vw_pass():
         for i in range(1, half):
             ci = lax.rem(chip + i, half)
             for c in range(2):
-                arrived(vwe.at[ci * 2 + c, rows_of(me_t, S)], vx_r.at[ci * 2 + c], vx_s.at[i, c])
-            piece = vw_piece(ci, me_t)
-            send(piece, piece, vwy_s.at[i, z], vw_r.at[ci, me_t], {"tok": ypart})
-            for d in range(1, Z):
-                send(piece, piece, vwz_s.at[i, d], vw_r.at[ci, me_t], {"tok": lax.rem(me_t + 2 * d, M)})
+                arrived(vwe.at[ci * 2 + c, vw_rows(y, g)], vx_r.at[ci * 2 + c], vx_s.at[i, c])
+            piece = vwe.at[pl.ds(ci * 2, 2), vw_rows(y, g)]
+            send(piece, piece, vwz_s.at[i], vwz_r.at[ci], {"tok": zpair})
+            send(piece, piece, vwy_s.at[i, 0], vwy_r.at[ci, 0], {"tok": ypart})
+
+    @scoped
+    def vw_turn():
+        for i in range(1, half):
+            ci = lax.rem(chip + i, half)
+            piece = vwe.at[pl.ds(ci * 2, 2), vw_rows(y, 1 - g)]
+            arrived(piece, vwz_r.at[ci], vwz_s.at[i])
+            send(piece, piece, vwy_s.at[i, 1], vwy_r.at[ci, 1], {"tok": ypart})
 
     def hid_piece(zz, side, p):
         return hida.at[zz, side, pl.ds(p * (T // 2), T // 2)]
 
-    def slab(v, t):
-        return pl.ds(pl.multiple_of(v * E + t * S, S), S)
-
-    for i in range(1, half):
-        for c in range(2):
-            v = lax.rem(chip + i, half) * 2 + c
-            send(vw.at[slab(v, me_t)], vwe.at[me_v, rows_of(me_t, S)],
-                 vx_s.at[i, c], vx_r.at[me_v], {"voc": v})
+    vw_send()
     for p in range(2):
         piece = hid_piece(z, core, p)
         send(piece, piece, hz_s.at[0, z, p], hz_r.at[z, p], {"tok": me_t + 2}, has_r)
@@ -523,7 +546,6 @@
     send(vw.at[rows_of(partner, E)], vwe.at[me_v], vp_s.at[0], vp_r.at[0], {"voc": partner})
     for c in range(chunks):
         unmix(c)
-    vw_own()
 
     def context(zz, k):
         both = jnp.dot(hida[zz, 0], w[k, 0:H, :], preferred_element_type=F32)
@@ -533,6 +555,8 @@
     for k in range(K):
         with jax.named_scope("context"):
             ctx[me_v, k * T:(k + 1) * T, :] = context(z, k)
+        if k == 1:
+            vw_pass()
         piece = ctx.at[me_v, pl.ds(k * T, T)]
         for i in range(1, half):
             send(piece, piece, ctx_s.at[i, k], ctx_r.at[me_v, k],
@@ -543,16 +567,6 @@
     def add_logits(s, first=False):
         part = jnp.dot(ctx[s], vw[rows_of(s, E), :], preferred_element_type=F32)
         logit[...] = part if first else logit[...] + part
-
-    @scoped
-    def relay_vw(j):
-        zz = mate(j)
-        t = zz * 2 + y
-        for i in range(1, half):
-            ci = lax.rem(chip + i, half)
-            piece = vw_piece(ci, t)
-            arrived(piece, vw_r.at[ci, t], vwy_s.at[i, zz])
-            send(piece, piece, vwy_s.at[i, zz], vw_r.at[ci, t], {"tok": ypart})
 
     @scoped
     def relay_hid(j, p, fwd):
@@ -619,13 +633,14 @@
         relay_hid(1, 0, False)
         relay_hid(1, 1, False)
     ctx_pass(1)
-    for j in range(1, Z):
-        relay_vw(j)
+    vw_turn()
     if Z > 1:
         ctx_mate(1, range(K))
+    for j in range(3, Z):
+        relay_hid(j, 0, True)
     ctx_pass(2)
     for j in range(3, Z):
-        relay_hid(j, 0, True)
+        relay_hid(j, 1, True)
     if Z > 2:
         relay_hid(2, 0, False)
     for k in range(3, K):
@@ -681,6 +696,9 @@
         rows = slice(k * T, (k + 1) * T)
         logit[rows, :] = jnp.exp(logit[rows, :] - column(logz[k:k + 1, :], V)) - onehot
         lgall[z, me_v, k] = logit[rows, :].astype(BF16)
+
+    @scoped
+    def own_share(k):
         share(z, k)
 
     @scoped
@@ -797,9 +815,8 @@
         arrived(vwe.at[partner], vp_r.at[0], vp_s.at[0])
         for i in range(1, half):
             ci = lax.rem(chip + i, half)
-            for zz in range(Z):
-                t = zz * 2 + 1 - y
-                arrived(vw_piece(ci, t), vw_r.at[ci, t], vwy_s.at[i, zz])
+            for p, part in enumerate((g, 1 - g)):
+                arrived(vwe.at[pl.ds(ci * 2, 2), vw_rows(1 - y, part)], vwy_r.at[ci, p], vwy_s.at[i, p])
         for s in range(N):
             vwt[s] = vwe[s].T
 
@@ -811,42 +828,22 @@
                 htr[b, :, zz * T:(zz + 1) * T] = hida[
                     zz, col // H, :, pl.ds(pl.multiple_of(col % H, R), R)].T
 
-    hid_order = list(range(1, N)) + [0]
-    events = []
-
-    def at(time, fn, *args):
-        events.append((time, len(events), fn, args))
-
-    late = [1.2 + 2.2 * (k - 1) if k else 0.0 for k in range(K)]
-    for k in range(K):
-        at(0.01 * k, own_out, k)
-        at(0.01 * k if k < 2 else 3.0 + 1.62 * (k - 2), own_line, k)
-        for j in range(1, Z):
-            at(late[k] + 2.2 * ((j + 1) // 2), relay_lg, k, j, True)
-        for j in range(1, Z):
-            at(late[k] + 2.2 * j, relay_lg, k, j, False)
-        for j in range(Z):
-            time = 2.2 * (j + 1) + (1.2 * k if j == 0 else 1.2 * late[k])
-            at(time, cross_lg, k, j)
-            at(time + (0.8 if j == Z - 1 else 1.2), pre_grad, k, j)
-        at(2.2 * Z + 1.2 * late[k] + 0.81, proj_part, k)
-        if k > 0:
-            for d in hid_order[(k - 1) * N // K:(k if k < K - 1 else K) * N // K]:
-                at(2.2 * Z + 1.2 * late[k] + 0.82, hid_send, d)
-    at(2.201, scales)
-    if Z > 2:
-        at(0.3, ctx_mate, 2, range(K))
-    at(2.202, vocab_part)
-    for j in range(3, Z):
-        at(0.2, relay_hid, j, 1, True)
-        at(2.25, relay_hid, j, 0, False)
-        at(3.35, relay_hid, j, 1, False)
-        at(4.5, ctx_mate, j, range(K))
-    at(2.21, vw_done)
-    at(4.6, turn)
-    at(13.5, pair_sums)
-    for _, _, fn, args in sorted(events, key=lambda e: e[:2]):
-        fn(*args)
+    def relay_on(k, j):
+        relay_lg(k, j, True)
+
+    def relay_in(k, j):
+        relay_lg(k, j, False)
+
+    def mate_ctx(j):
+        ctx_mate(j, range(K))
+
+    def hid_in(j, p):
+        relay_hid(j, p, False)
+
+    steps = (own_out, own_share, own_line, relay_on, relay_in, cross_lg, pre_grad, proj_part,
+             scales, vocab_part, mate_ctx, hid_in, vw_done, turn, hid_send, pair_sums)
+    for step, *rest in ORDER:
+        steps[step](*rest)
 
     vtot = vsum[...]
     for d in range(1, Z):
@@ -911,7 +908,7 @@
         dma((half, K)), dma((half, K)), dma((N, K)), dma((N,)), dma((N,)),
         dma((2, Z, 2)), dma((Z, 2)), dma((Z, 2)), dma((Z, 2)),
         dma((half, 2)), dma((N,)), dma((1,)), dma((1,)),
-        dma((half, Z)), dma((half, Z)), dma((half, M)), dma((N,)), dma((N,)),
+        dma((half,)), dma((half,)), dma((half, 2)), dma((half, 2)), dma((N,)), dma((N,)),
         dma((2, Z, K)), dma((half, Z, K)), dma((half, Z, K)), dma((Z, N, K)),
         dma((Z,)), dma((Z,)), dma((Z,)), dma((Z,)), dma((N,)), dma((N,)),
         dma((K + 1,)), dma((K + 1,)), dma((Z,)), dma((Z,)),
@@ -966,7 +963,7 @@
     K, E = mix_weight.shape
     V = vocab_weight.shape[1]
     gathered = 2 * (M // 2) * T * (K * N * V + D + 2 * K * E)
-    shapes = K == 4 and E % 128 == 0 and (E // M) % 16 == 0 and (D // M) % (256 // K) == 0
+    shapes = K == 4 and M == 8 and N == 4 and E % 128 == 0 and (D // M) % (256 // K) == 0
     if shapes and gathered + 4 * K * D * E <= 28 * 1024 * 1024:
         return body_fast(M, N, *args)
     return body_base(M, N, *args)

time: 74.3 us -> 71.1 us (0.957)
  Pallas kernels: 73.3 us -> 70.2 us
    pallas_call x1, Pallas kernels: 72.2 us -> 69.1 us  [body_fast(): pl.pallas_call(functools.partial(fast_kernel, M, N), out_shape=(jax.Shape...]
where the time goes in v3:
time: 71.1 us; the launch traced here: 71 us
  Pallas kernels  70.2 us (99%)
  between operations  0.8 us (1%)
    pallas_call x1, Pallas kernels, body_fast(): pl.pallas_call(functools.partial(fast_kernel, M, N), out_shape=(jax.Shape...  69.1 us

profile of v3, /device:TPU:0, one launch (start us, length us, event | category | flops | bytes accessed | tf_op | source)
XLA Modules:
  0.0 71.0 jit_solution(15768015369372321067)
XLA Ops:
  0.6 69.1 %shard_map.94 = (bf16[128,512]{1,0:T(8,128)(2,1)S(1)}, bf16[4,256,4,128]{3,2,1,0:T(4,128)(2,1)S(1)}, bf16[256,256]{1,0:T(8,128)(2,1)S(1)}) custom-call(bf16[128,2048]{1,0:T(8,128)(2,1)} %hid_hbm.1, bf16[4,512]{1,0:T(4,128)(2,1)} %mix_hbm.1, bf16[2048,4,512]{2,1,0:T(4,128)(2,1)} %proj_hbm.1, bf16[2048,256]{1,0:T(8,128)(2,1)} %vw_hbm.1, f32[4,128]{1,0:T(4,128)} %logz_hbm.1, ...), custom_call_target="tpu_custom_call" | custom-call | tf_op jit(solution)/shard_map/pallas_call | solution.py:918
  69.7 1.1 %shard_map.95 = (bf16[128,512]{1,0:T(8,128)(2,1)}, bf16[256,4,512]{2,1,0:T(4,128)(2,1)}, bf16[256,256]{1,0:T(8,128)(2,1)}) custom-call(bf16[128,512]{1,0:T(8,128)(2,1)S(1)} %get-tuple-element.6.hid, bf16[4,256,4,128]{3,2,1,0:T(4,128)(2,1)S(1)} %get-tuple-element.7.proj, bf16[256,256]{1,0:T(8,128)(2,1)S(1)} %get-tuple-element.8.voc), custom_call_target="tpu_custom_call" | custom-call | tf_op jit(solution)/shard_map/pallas_call | solution.py:935

commit v4 on v3

--- a/solution.py
+++ b/solution.py
@@ -362,15 +362,15 @@
 
 
 ORDER = (
-    (0, 0), (0, 2), (2, 0), (11, 3, 0), (0, 1), (2, 1), (1, 1), (1, 2), (10, 2), (0, 3), (1, 0), (8,),
-    (3, 0, 2), (3, 0, 1), (9,), (3, 0, 3), (4, 0, 1), (3, 1, 1), (4, 1, 1), (11, 3, 1), (4, 0, 2),
-    (3, 1, 2), (2, 2), (12,), (4, 0, 3), (10, 3), (4, 1, 2), (5, 0, 2), (1, 3), (5, 0, 1), (5, 0, 0),
-    (13,), (3, 1, 3), (2, 3), (6, 0, 2), (5, 0, 3), (5, 1, 0), (6, 0, 1), (6, 0, 0), (3, 2, 1), (3, 2, 2),
-    (4, 1, 3), (4, 2, 1), (5, 1, 1), (6, 0, 3), (7, 0), (4, 2, 2), (5, 2, 0), (3, 2, 3), (5, 1, 2),
-    (3, 3, 2), (3, 3, 1), (6, 1, 0), (5, 3, 0), (4, 2, 3), (5, 1, 3), (6, 1, 1), (4, 3, 2), (6, 1, 2),
-    (6, 1, 3), (7, 1), (3, 3, 3), (4, 3, 1), (5, 2, 3), (4, 3, 3), (5, 2, 1), (5, 2, 2), (6, 3, 0),
-    (6, 2, 2), (6, 2, 0), (5, 3, 1), (6, 2, 3), (15,), (5, 3, 2), (6, 2, 1), (7, 2), (5, 3, 3), (6, 3, 1),
-    (14, 1), (6, 3, 2), (6, 3, 3), (7, 3), (14, 0), (14, 2), (14, 3),
+    (0, 0), (1, 0), (2, 0), (0, 1), (2, 1), (12,), (0, 2), (1, 1), (0, 3), (1, 3), (10, 2), (8,), (9,),
+    (1, 2), (3, 0, 1), (3, 0, 2), (3, 0, 3), (11, 3, 0), (3, 1, 1), (2, 3), (4, 0, 3), (4, 0, 1),
+    (3, 1, 2), (11, 3, 1), (2, 2), (10, 3), (5, 0, 0), (4, 0, 2), (4, 1, 1), (5, 2, 0), (13,), (5, 0, 1),
+    (4, 3, 1), (3, 1, 3), (3, 3, 2), (3, 3, 1), (6, 0, 1), (5, 0, 3), (6, 0, 0), (5, 0, 2), (4, 1, 2),
+    (5, 1, 0), (6, 0, 3), (6, 0, 2), (7, 0), (4, 1, 3), (4, 2, 1), (3, 3, 3), (5, 1, 1), (4, 3, 2),
+    (3, 2, 1), (5, 1, 2), (5, 1, 3), (3, 2, 2), (5, 3, 0), (6, 1, 0), (6, 1, 1), (5, 3, 1), (6, 1, 2),
+    (3, 2, 3), (4, 3, 3), (6, 1, 3), (7, 1), (6, 2, 0), (4, 2, 2), (6, 3, 1), (6, 3, 0), (5, 3, 2), (15,),
+    (4, 2, 3), (5, 3, 3), (6, 3, 2), (5, 2, 1), (5, 2, 2), (6, 3, 3), (7, 3), (5, 2, 3), (6, 2, 2),
+    (6, 2, 1), (6, 2, 3), (7, 2), (14, 0), (14, 1), (14, 2), (14, 3),
 )
 
 
@@ -398,7 +398,7 @@
     vgb, vgy, vsum, vout, vin, hss, hsr, own_hs, acc, psend, precv, mgrad,
     l_sem, w_sem, ctx_s, ctx_f, ctx_r, mix_s, mix_r, hz_s, hz_r, hp_s, hp_r,
     vx_s, vx_r, vp_s, vp_r, vwz_s, vwz_r, vwy_s, vwy_r, tgt_s, tgt_r,
-    lz_s, lx_s, lp_s, lg_r, vy_s, vy_r, vz_s, vz_r, hs_s, hs_r, pp_s, pp_r, sc_s, sc_r,
+    lz_s, lx_s, lp_s, lg_r, vy_s, vy_r, vz_s, vz_r, hs_s, hs_r, pp_s, pp_r, sc_s, sc_r, le_s,
 ):
     K, D, E = w.shape
     T = hida.shape[2]
@@ -468,8 +468,13 @@
         pltpu.make_async_copy(tg_hbm, targets, l_sem.at[5]),
         pltpu.make_async_copy(loss_hbm, loss, l_sem.at[6]),
     ]
-    for c in loads:
+    loads[0].start()
+    loads[1].start()
+    loads[2].start()
+    for c in loads[3:]:
         c.start()
+    for j in range(J):
+        w_copy(0, j).start()
 
     bar = pltpu.get_barrier_semaphore()
     for d in range(1, M):
@@ -493,7 +498,7 @@
     with jax.named_scope("loads"):
         for c in loads[:3]:
             c.wait()
-    for c in range(chunks):
+    for c in range(1, chunks):
         for j in range(J):
             w_copy(c, j).start()
     with jax.named_scope("barrier"):
@@ -706,11 +711,17 @@
         piece = lgall.at[z, me_v, k]
         send(piece, piece, lz_s.at[0, z, k], lg_r.at[z, me_v, k], {"tok": me_t + 2}, has_r)
         send(piece, piece, lz_s.at[1, z, k], lg_r.at[z, me_v, k], {"tok": me_t - 2}, has_l)
+        if k == 0:
+            send(piece, piece, le_s.at[0], lg_r.at[z, me_v, k], {"tok": me_t + M - 2}, z == 0)
+            send(piece, piece, le_s.at[1], lg_r.at[z, me_v, k], {"tok": me_t - M + 2}, z == Z - 1)
 
     @scoped
     def relay_lg(k, j, fwd):
         zz = mate(j)
         there, to = onward(zz)
+        if k == 0:
+            end = to // 2
+            there = there & (end - zz < Z - 1) & (zz - end < Z - 1)
         piece = lgall.at[zz, me_v, k]
         on = remote(piece, piece, lz_s.at[0, zz, k], lg_r.at[zz, me_v, k], {"tok": to})
 
@@ -805,9 +816,9 @@
         for s in range(N):
             vgb[s * E:(s + 1) * E, :] = lax.dot_general(
                 ctx[s], lg[...], TN, preferred_element_type=F32).astype(BF16)
-        for zz in range(Z):
-            send(vgb.at[pl.ds((zz * 2 + 1 - y) * R, R)], vgy.at[zz], vy_s.at[zz], vy_r.at[zz],
-                 {"tok": ypart})
+            for zz in range(s * Z // N, (s + 1) * Z // N):
+                send(vgb.at[pl.ds((zz * 2 + 1 - y) * R, R)], vgy.at[zz], vy_s.at[zz], vy_r.at[zz],
+                     {"tok": ypart})
 
     @scoped
     def vw_done():
@@ -911,7 +922,7 @@
         dma((half,)), dma((half,)), dma((half, 2)), dma((half, 2)), dma((N,)), dma((N,)),
         dma((2, Z, K)), dma((half, Z, K)), dma((half, Z, K)), dma((Z, N, K)),
         dma((Z,)), dma((Z,)), dma((Z,)), dma((Z,)), dma((N,)), dma((N,)),
-        dma((K + 1,)), dma((K + 1,)), dma((Z,)), dma((Z,)),
+        dma((K + 1,)), dma((K + 1,)), dma((Z,)), dma((Z,)), dma((2,)),
     ]
     spec = pl.BlockSpec(memory_space=pltpu.VMEM)
     hbm = pl.BlockSpec(memory_space=pltpu.MemorySpace.HBM)

time: 71.1 us -> 70 us (0.985)
  Pallas kernels: 70.2 us -> 69.1 us
    pallas_call x1, Pallas kernels: 69.1 us -> 68 us  [body_fast(): pl.pallas_call(functools.partial(fast_kernel, M, N), out_shape=(jax.Shape...]
where the time goes in v4:
time: 70 us; the launch traced here: 69.9 us
  Pallas kernels  69.1 us (99%)
  between operations  0.8 us (1%)
    pallas_call x1, Pallas kernels, body_fast(): pl.pallas_call(functools.partial(fast_kernel, M, N), out_shape=(jax.Shape...  68 us

profile of v4, /device:TPU:0, one launch (start us, length us, event | category | flops | bytes accessed | tf_op | source)
XLA Modules:
  0.0 69.9 jit_solution(5305252350549870694)
XLA Ops:
  0.6 68.0 %shard_map.94 = (bf16[128,512]{1,0:T(8,128)(2,1)S(1)}, bf16[4,256,4,128]{3,2,1,0:T(4,128)(2,1)S(1)}, bf16[256,256]{1,0:T(8,128)(2,1)S(1)}) custom-call(bf16[128,2048]{1,0:T(8,128)(2,1)} %hid_hbm.1, bf16[4,512]{1,0:T(4,128)(2,1)} %mix_hbm.1, bf16[2048,4,512]{2,1,0:T(4,128)(2,1)} %proj_hbm.1, bf16[2048,256]{1,0:T(8,128)(2,1)} %vw_hbm.1, f32[4,128]{1,0:T(4,128)} %logz_hbm.1, ...), custom_call_target="tpu_custom_call" | custom-call | tf_op jit(solution)/shard_map/pallas_call | solution.py:929
  68.6 1.1 %shard_map.95 = (bf16[128,512]{1,0:T(8,128)(2,1)}, bf16[256,4,512]{2,1,0:T(4,128)(2,1)}, bf16[256,256]{1,0:T(8,128)(2,1)}) custom-call(bf16[128,512]{1,0:T(8,128)(2,1)S(1)} %get-tuple-element.6.hid, bf16[4,256,4,128]{3,2,1,0:T(4,128)(2,1)S(1)} %get-tuple-element.7.proj, bf16[256,256]{1,0:T(8,128)(2,1)S(1)} %get-tuple-element.8.voc), custom_call_target="tpu_custom_call" | custom-call | tf_op jit(solution)/shard_map/pallas_call | solution.py:946

commit v5 on v4

--- a/solution.py
+++ b/solution.py
@@ -1,4 +1,5 @@
 import functools
+import math
 
 import jax
 import jax.numpy as jnp
@@ -396,9 +397,9 @@
     raw, w, hida, vw, vwe, vwt, mix, logz, targets, loss,
     ctx, ctxz, mix_all, htr, logit, lg, lgall, tgt, scale, pg,
     vgb, vgy, vsum, vout, vin, hss, hsr, own_hs, acc, psend, precv, mgrad,
-    l_sem, w_sem, ctx_s, ctx_f, ctx_r, mix_s, mix_r, hz_s, hz_r, hp_s, hp_r,
-    vx_s, vx_r, vp_s, vp_r, vwz_s, vwz_r, vwy_s, vwy_r, tgt_s, tgt_r,
-    lz_s, lx_s, lp_s, lg_r, vy_s, vy_r, vz_s, vz_r, hs_s, hs_r, pp_s, pp_r, sc_s, sc_r, le_s,
+    l_sem, w_sem, all_s, over_s, own_s, on_s,
+    ctx_r, mix_r, hz_r, hp_r, vx_r, vp_r, vwz_r, vwy_r,
+    tgt_r, lg_r, vy_r, vz_r, hs_r, pp_r, sc_r,
 ):
     K, D, E = w.shape
     T = hida.shape[2]
@@ -419,7 +420,6 @@
     ypart = me_t + 1 - 2 * y
     has_r = z + 1 < Z
     has_l = z >= 1
-    sends = []
 
     def remote(src, dst, ss, rs, dev):
         return pltpu.make_async_remote_copy(
@@ -427,16 +427,21 @@
             device_id=dev, device_id_type=MESH,
         )
 
-    def send(src, dst, ss, rs, dev, pred=None):
-        c = remote(src, dst, ss, rs, dev)
-        if pred is None:
-            c.start()
-        else:
-            pl.when(pred)(c.start)
-        sends.append((pred, c))
-
-    def arrived(ref, rs, ss):
-        remote(ref, ref, ss, rs, {"voc": partner}).wait_recv()
+    groups = [0]
+
+    def send(src, dst, rs, dev):
+        size = math.prod(src.shape) * jnp.dtype(src.dtype).itemsize
+        if groups[-1] + size > D * K * 256:
+            groups.append(0)
+        groups[-1] += size
+        remote(src, dst, all_s.at[len(groups) - 1], rs, dev).start()
+
+    def sent(sem, size):
+        ref = raw.at[0, pl.ds(0, size // (K * 256))]
+        remote(ref, ref, sem, vp_r.at[0], {"voc": partner}).wait_send()
+
+    def arrived(ref, rs):
+        remote(ref, ref, all_s.at[0], rs, {"voc": partner}).wait_recv()
 
     def mate(j):
         if j == 0:
@@ -457,7 +462,7 @@
     def w_copy(c, j):
         return pltpu.make_async_copy(
             proj_hbm.at[pl.ds(c * n, n), :, pl.ds(j * 128, 128)],
-            raw.at[j, pl.ds(c * n, n)], w_sem.at[c, j])
+            raw.at[j, pl.ds(c * n, n)], w_sem.at[c])
 
     loads = [
         pltpu.make_async_copy(hid_hbm.at[:, pl.ds(0, H)], hida.at[z, 0], l_sem.at[0]),
@@ -486,8 +491,8 @@
 
     @scoped
     def unmix(c):
-        for j in range(J):
-            w_copy(c, j).wait()
+        chunk = raw.at[:, pl.ds(c * n, n)]
+        pltpu.make_async_copy(chunk, chunk, w_sem.at[c]).wait()
         for b in range(c * n // B, (c + 1) * n // B):
             x = jnp.concatenate(
                 [raw.at[j].reshape(D * K, 128)[b * 256:(b + 1) * 256, :] for j in range(J)], axis=1)
@@ -516,25 +521,25 @@
                 v = lax.rem(chip + i, half) * 2 + c
                 rows = vw_rows(y, g)
                 send(vw.at[pl.ds(pl.multiple_of(v * E + rows.start, E // 4), rows.size)],
-                     vwe.at[me_v, rows], vx_s.at[i, c], vx_r.at[me_v], {"voc": v})
+                     vwe.at[me_v, rows], vx_r.at[me_v], {"voc": v})
 
     @scoped
     def vw_pass():
         for i in range(1, half):
             ci = lax.rem(chip + i, half)
             for c in range(2):
-                arrived(vwe.at[ci * 2 + c, vw_rows(y, g)], vx_r.at[ci * 2 + c], vx_s.at[i, c])
+                arrived(vwe.at[ci * 2 + c, vw_rows(y, g)], vx_r.at[ci * 2 + c])
             piece = vwe.at[pl.ds(ci * 2, 2), vw_rows(y, g)]
-            send(piece, piece, vwz_s.at[i], vwz_r.at[ci], {"tok": zpair})
-            send(piece, piece, vwy_s.at[i, 0], vwy_r.at[ci, 0], {"tok": ypart})
+            send(piece, piece, vwz_r.at[ci], {"tok": zpair})
+            send(piece, piece, vwy_r.at[ci, 0], {"tok": ypart})
 
     @scoped
     def vw_turn():
         for i in range(1, half):
             ci = lax.rem(chip + i, half)
             piece = vwe.at[pl.ds(ci * 2, 2), vw_rows(y, 1 - g)]
-            arrived(piece, vwz_r.at[ci], vwz_s.at[i])
-            send(piece, piece, vwy_s.at[i, 1], vwy_r.at[ci, 1], {"tok": ypart})
+            arrived(piece, vwz_r.at[ci])
+            send(piece, piece, vwy_r.at[ci, 1], {"tok": ypart})
 
     def hid_piece(zz, side, p):
         return hida.at[zz, side, pl.ds(p * (T // 2), T // 2)]
@@ -542,13 +547,13 @@
     vw_send()
     for p in range(2):
         piece = hid_piece(z, core, p)
-        send(piece, piece, hz_s.at[0, z, p], hz_r.at[z, p], {"tok": me_t + 2}, has_r)
-        send(piece, piece, hz_s.at[1, z, p], hz_r.at[z, p], {"tok": me_t - 2}, has_l)
+        pl.when(has_r)(remote(piece, piece, own_s.at[0], hz_r.at[z, p], {"tok": me_t + 2}).start)
+        pl.when(has_l)(remote(piece, piece, own_s.at[1], hz_r.at[z, p], {"tok": me_t - 2}).start)
     for c in loads[3:]:
         c.wait()
     for d in range(1, N):
-        send(mix, mix_all.at[d], mix_s.at[d], mix_r.at[d], {"voc": lax.rem(me_v + d, N)})
-    send(vw.at[rows_of(partner, E)], vwe.at[me_v], vp_s.at[0], vp_r.at[0], {"voc": partner})
+        send(mix, mix_all.at[d], mix_r.at[d], {"voc": lax.rem(me_v + d, N)})
+    send(vw.at[rows_of(partner, E)], vwe.at[me_v], vp_r.at[0], {"voc": partner})
     for c in range(chunks):
         unmix(c)
 
@@ -564,9 +569,9 @@
             vw_pass()
         piece = ctx.at[me_v, pl.ds(k * T, T)]
         for i in range(1, half):
-            send(piece, piece, ctx_s.at[i, k], ctx_r.at[me_v, k],
+            send(piece, piece, ctx_r.at[me_v, k],
                  {"voc": lax.rem(chip + i, half) * 2 + core})
-        send(piece, piece, ctx_s.at[0, k], ctx_r.at[me_v, k], {"voc": partner})
+        send(piece, piece, ctx_r.at[me_v, k], {"voc": partner})
 
     @scoped
     def add_logits(s, first=False):
@@ -578,25 +583,22 @@
         zz = mate(j)
         there, to = onward(zz)
         piece = hid_piece(zz, core, p)
-        on = remote(piece, piece, hz_s.at[0, zz, p], hz_r.at[zz, p], {"tok": to})
-        over = remote(piece, piece, hp_s.at[zz, p], hp_r.at[zz, p], {"voc": partner})
+        on = remote(piece, piece, on_s.at[0, j], hz_r.at[zz, p], {"tok": to})
+        over = remote(piece, piece, over_s.at[0], hp_r.at[zz, p], {"voc": partner})
 
         @pl.when(there if fwd else jnp.logical_not(there))
         def _():
-            arrived(piece, hz_r.at[zz, p], hz_s.at[0, zz, p])
+            arrived(piece, hz_r.at[zz, p])
             if fwd:
                 on.start()
             over.start()
-        if fwd:
-            sends.append((there, on))
-            sends.append((None, over))
 
     @scoped
     def ctx_mate(j, ks):
         zz = mate(j)
         if ks[0] == 0:
             for p in range(2):
-                arrived(hid_piece(zz, 1 - core, p), hp_r.at[zz, p], hp_s.at[zz, p])
+                arrived(hid_piece(zz, 1 - core, p), hp_r.at[zz, p])
         for k in ks:
             ctxz[zz, k * T:(k + 1) * T, :] = context(zz, k)
 
@@ -605,14 +607,14 @@
         for i in range(1, half):
             s = lax.rem(chip - i + half, half) * 2 + core
             piece = ctx.at[s, pl.ds(k * T, T)]
-            arrived(piece, ctx_r.at[s, k], ctx_s.at[i, k])
-            send(piece, piece, ctx_f.at[i, k], ctx_r.at[s, k], {"voc": partner})
+            arrived(piece, ctx_r.at[s, k])
+            send(piece, piece, ctx_r.at[s, k], {"voc": partner})
 
     add_logits(me_v, True)
     for j in range(1, min(Z, 3)):
         relay_hid(j, 0, True)
     for k in range(K):
-        arrived(ctx.at[partner, pl.ds(k * T, T)], ctx_r.at[partner, k], ctx_s.at[0, k])
+        arrived(ctx.at[partner, pl.ds(k * T, T)], ctx_r.at[partner, k])
     add_logits(partner)
 
     tcol = column(targets[...].astype(F32), V)
@@ -620,7 +622,7 @@
     onehot = (tcol == ids).astype(F32)
     mix_all[0] = mix[...]
     for d in range(1, N):
-        arrived(mix_all.at[d], mix_r.at[d], mix_s.at[d])
+        arrived(mix_all.at[d], mix_r.at[d])
     mixing = jnp.zeros((K, T), F32)
     for d in range(N):
         s = lax.rem(me_v - d + N, N)
@@ -657,7 +659,7 @@
     for i in range(1, half):
         s = lax.rem(chip - i + half, half) * 2 + 1 - core
         for k in range(K):
-            arrived(ctx.at[s, pl.ds(k * T, T)], ctx_r.at[s, k], ctx_s.at[i, k])
+            arrived(ctx.at[s, pl.ds(k * T, T)], ctx_r.at[s, k])
         add_logits(s)
 
     lane = lax.broadcasted_iota(jnp.int32, (T, 128), 1)
@@ -667,11 +669,11 @@
         table = jnp.where(lane == k, part, table)
     tgt[0] = table.T[0:8, :]
     for d in range(1, N):
-        send(tgt.at[0], tgt.at[d], tgt_s.at[d], tgt_r.at[d], {"voc": lax.rem(me_v + d, N)})
+        send(tgt.at[0], tgt.at[d], tgt_r.at[d], {"voc": lax.rem(me_v + d, N)})
     @scoped
     def scales():
         for d in range(1, N):
-            arrived(tgt.at[d], tgt_r.at[d], tgt_s.at[d])
+            arrived(tgt.at[d], tgt_r.at[d])
         target = tgt[0]
         for d in range(1, N):
             target = target + tgt[d]
@@ -681,20 +683,19 @@
         scale[z, 0:K, :] = loss[...] * posterior
         mgrad[...] = loss[...] * (weights - posterior)
         for d in range(1, Z):
-            send(scale.at[z], scale.at[z], sc_s.at[d], sc_r.at[z], {"tok": lax.rem(me_t + 2 * d, M)})
+            send(scale.at[z], scale.at[z], sc_r.at[z], {"tok": lax.rem(me_t + 2 * d, M)})
 
     def shares(zz, k):
         piece = lgall.at[zz, me_v, k]
         return [
-            remote(piece, piece, lx_s.at[i, zz, k], lg_r.at[zz, me_v, k],
+            remote(piece, piece, over_s.at[1], lg_r.at[zz, me_v, k],
                    {"voc": lax.rem(chip + i, half) * 2 + core})
             for i in range(1, half)
-        ] + [remote(piece, piece, lp_s.at[0, zz, k], lg_r.at[zz, me_v, k], {"voc": partner})]
+        ] + [remote(piece, piece, over_s.at[2], lg_r.at[zz, me_v, k], {"voc": partner})]
 
     def share(zz, k):
         for c in shares(zz, k):
             c.start()
-            sends.append((None, c))
 
     @scoped
     def own_out(k):
@@ -709,33 +710,33 @@
     @scoped
     def own_line(k):
         piece = lgall.at[z, me_v, k]
-        send(piece, piece, lz_s.at[0, z, k], lg_r.at[z, me_v, k], {"tok": me_t + 2}, has_r)
-        send(piece, piece, lz_s.at[1, z, k], lg_r.at[z, me_v, k], {"tok": me_t - 2}, has_l)
+        pl.when(has_r)(remote(piece, piece, own_s.at[0], lg_r.at[z, me_v, k], {"tok": me_t + 2}).start)
+        pl.when(has_l)(remote(piece, piece, own_s.at[1], lg_r.at[z, me_v, k], {"tok": me_t - 2}).start)
         if k == 0:
-            send(piece, piece, le_s.at[0], lg_r.at[z, me_v, k], {"tok": me_t + M - 2}, z == 0)
-            send(piece, piece, le_s.at[1], lg_r.at[z, me_v, k], {"tok": me_t - M + 2}, z == Z - 1)
+            for way, end in ((0, 0), (1, Z - 1)):
+                far = remote(piece, piece, own_s.at[2 + way], lg_r.at[z, me_v, k],
+                             {"tok": me_t + (1 - 2 * way) * (M - 2)})
+                pl.when(z == end)(far.start)
+
+    def near_end(zz, there, to):
+        end = to // 2
+        return there & (end - zz < Z - 1) & (zz - end < Z - 1)
 
     @scoped
     def relay_lg(k, j, fwd):
         zz = mate(j)
         there, to = onward(zz)
         if k == 0:
-            end = to // 2
-            there = there & (end - zz < Z - 1) & (zz - end < Z - 1)
+            there = near_end(zz, there, to)
         piece = lgall.at[zz, me_v, k]
-        on = remote(piece, piece, lz_s.at[0, zz, k], lg_r.at[zz, me_v, k], {"tok": to})
+        on = remote(piece, piece, on_s.at[1 if k == 0 else 0, j], lg_r.at[zz, me_v, k], {"tok": to})
 
         @pl.when(there if fwd else jnp.logical_not(there))
         def _():
-            arrived(piece, lg_r.at[zz, me_v, k], lp_s.at[0, zz, k])
+            arrived(piece, lg_r.at[zz, me_v, k])
             if fwd:
                 on.start()
-            for c in shares(zz, k):
-                c.start()
-        if fwd:
-            sends.append((there, on))
-            for c in shares(zz, k):
-                sends.append((None, c))
+            share(zz, k)
 
     @scoped
     def cross_lg(k, j):
@@ -743,8 +744,8 @@
         for i in range(1, half):
             s = lax.rem(chip - i + half, half) * 2 + core
             piece = lgall.at[zz, s, k]
-            arrived(piece, lg_r.at[zz, s, k], lp_s.at[0, zz, k])
-            send(piece, piece, lp_s.at[i, zz, k], lg_r.at[zz, s, k], {"voc": partner})
+            arrived(piece, lg_r.at[zz, s, k])
+            remote(piece, piece, over_s.at[3], lg_r.at[zz, s, k], {"voc": partner}).start()
 
     @scoped
     def pre_grad(k, j):
@@ -752,7 +753,7 @@
         rows = slice(k * T, (k + 1) * T)
         for i in range(half):
             s = lax.rem(chip + i, half) * 2 + 1 - core
-            arrived(lgall.at[zz, s, k], lg_r.at[zz, s, k], lp_s.at[0, zz, k])
+            arrived(lgall.at[zz, s, k], lg_r.at[zz, s, k])
         total = None
         for s in range(N):
             part = jnp.dot(lgall[zz, s, k], vwt[s], preferred_element_type=F32)
@@ -760,7 +761,7 @@
         c = (ctx[me_v, rows, :] if j == 0 else ctxz[zz, rows, :]).astype(F32)
         if k == 0:
             if j > 0:
-                arrived(scale.at[zz], sc_r.at[zz], sc_s.at[1])
+                arrived(scale.at[zz], sc_r.at[zz])
         total = total * column(scale[zz, k:k + 1, :], E)
         pg[k, rows_of(zz, T), :] = (total * (1.0 - c * c)).astype(BF16)
 
@@ -779,19 +780,19 @@
             own_hs[...] = hid_part(s)
         else:
             hss[d] = hid_part(s).astype(BF16)
-            send(hss.at[d], hsr.at[d], hs_s.at[d], hs_r.at[d], {"voc": s})
+            send(hss.at[d], hsr.at[d], hs_r.at[d], {"voc": s})
 
     @scoped
     def pair_sums():
         for d in list(range(1, Z)) + [0]:
             zz = lax.rem(z + d, Z)
-            arrived(vgy.at[zz], vy_r.at[zz], vy_s.at[zz])
+            arrived(vgy.at[zz], vy_r.at[zz])
             total = vgb[rows_of(zz * 2 + y, R), :].astype(F32) + vgy[zz].astype(F32)
             if d == 0:
                 vsum[...] = total
             else:
                 vout[zz] = total.astype(BF16)
-                send(vout.at[zz], vin.at[z], vz_s.at[d], vz_r.at[z], {"tok": zz * 2 + y})
+                send(vout.at[zz], vin.at[z], vz_r.at[z], {"tok": zz * 2 + y})
 
     pieces = [(k, 0, E) for k in range(K)]
     if E % 256 == 0:
@@ -805,7 +806,7 @@
                 psend[k, :, lanes] = jnp.dot(
                     htr[1 - y], pg[k, :, lanes], preferred_element_type=F32).astype(BF16)
                 send(psend.at[k, :, pl.ds(lo, wide)], precv.at[k, :, pl.ds(lo, wide)],
-                     pp_s.at[p], pp_r.at[p], {"tok": ypart})
+                     pp_r.at[p], {"tok": ypart})
         acc[k] = jnp.dot(htr[y], pg[k], preferred_element_type=F32)
 
     @scoped
@@ -817,17 +818,17 @@
             vgb[s * E:(s + 1) * E, :] = lax.dot_general(
                 ctx[s], lg[...], TN, preferred_element_type=F32).astype(BF16)
             for zz in range(s * Z // N, (s + 1) * Z // N):
-                send(vgb.at[pl.ds((zz * 2 + 1 - y) * R, R)], vgy.at[zz], vy_s.at[zz], vy_r.at[zz],
+                send(vgb.at[pl.ds((zz * 2 + 1 - y) * R, R)], vgy.at[zz], vy_r.at[zz],
                      {"tok": ypart})
 
     @scoped
     def vw_done():
         vwe[me_v] = vw[rows_of(me_v, E), :]
-        arrived(vwe.at[partner], vp_r.at[0], vp_s.at[0])
+        arrived(vwe.at[partner], vp_r.at[0])
         for i in range(1, half):
             ci = lax.rem(chip + i, half)
             for p, part in enumerate((g, 1 - g)):
-                arrived(vwe.at[pl.ds(ci * 2, 2), vw_rows(1 - y, part)], vwy_r.at[ci, p], vwy_s.at[i, p])
+                arrived(vwe.at[pl.ds(ci * 2, 2), vw_rows(1 - y, part)], vwy_r.at[ci, p])
         for s in range(N):
             vwt[s] = vwe[s].T
 
@@ -859,12 +860,12 @@
     vtot = vsum[...]
     for d in range(1, Z):
         zz = lax.rem(z + d, Z)
-        arrived(vin.at[zz], vz_r.at[zz], vz_s.at[d])
+        arrived(vin.at[zz], vz_r.at[zz])
         vtot = vtot + vin[zz].astype(F32)
     out_vocab[...] = vtot.astype(BF16)
     htot = own_hs[...]
     for d in range(1, N):
-        arrived(hsr.at[d], hs_r.at[d], hs_s.at[d])
+        arrived(hsr.at[d], hs_r.at[d])
         htot = htot + hsr[d].astype(F32)
     mixf = mix[...].astype(F32)
     for k in range(K):
@@ -875,7 +876,7 @@
     for p, (k, lo, wide) in enumerate(pieces):
         lanes = slice(lo, lo + wide)
         with jax.named_scope("precv"):
-            arrived(precv.at[k, :, pl.ds(lo, wide)], pp_r.at[p], pp_s.at[p])
+            arrived(precv.at[k, :, pl.ds(lo, wide)], pp_r.at[p])
         psum = (acc[k, :, lanes] + precv[k, :, lanes].astype(F32)).astype(BF16)
         if k < K - 1:
             precv[k, :, lanes] = psum
@@ -888,11 +889,22 @@
                 out_proj.at[lo // 128 + j].reshape(R * K, 128)[b * 256:(b + 1) * 256, :] = (
                     out[:, j * 128:(j + 1) * 128])
     with jax.named_scope("drain"):
-        for pred, c in sends:
-            if pred is None:
-                c.wait_send()
-            else:
-                pl.when(pred)(c.wait_send)
+        for i, size in enumerate(groups):
+            sent(all_s.at[i], size)
+        piece = T * V * 2
+        sent(over_s.at[0], (Z - 1) * T * D)
+        for i in range(1, 4):
+            for _ in range(half - 1):
+                sent(over_s.at[i], Z * K * piece)
+        for way, pred in ((0, has_r), (1, has_l)):
+            pl.when(pred)(functools.partial(sent, own_s.at[way], T * D + K * piece))
+        for way, end in ((0, 0), (1, Z - 1)):
+            pl.when(z == end)(functools.partial(sent, own_s.at[2 + way], piece))
+        for j in range(1, Z):
+            zz = mate(j)
+            there, to = onward(zz)
+            pl.when(there)(functools.partial(sent, on_s.at[0, j], T * D + (K - 1) * piece))
+            pl.when(near_end(zz, there, to))(functools.partial(sent, on_s.at[1, j], piece))
 
 
 def body_fast(M, N, hidden, mix_weight, comp_proj, vocab_weight, log_normalizer, targets, loss_grad):
@@ -915,14 +927,9 @@
         vm((N, T, E), BF16), vm((N, T, E), BF16),
         vm((T, E), F32), vm((K, R, E), F32), vm((K, R, E), BF16), vm((K, R, E), BF16),
         vm((K, T), F32),
-        dma((7,)), dma((4, J)),
-        dma((half, K)), dma((half, K)), dma((N, K)), dma((N,)), dma((N,)),
-        dma((2, Z, 2)), dma((Z, 2)), dma((Z, 2)), dma((Z, 2)),
-        dma((half, 2)), dma((N,)), dma((1,)), dma((1,)),
-        dma((half,)), dma((half,)), dma((half, 2)), dma((half, 2)), dma((N,)), dma((N,)),
-        dma((2, Z, K)), dma((half, Z, K)), dma((half, Z, K)), dma((Z, N, K)),
-        dma((Z,)), dma((Z,)), dma((Z,)), dma((Z,)), dma((N,)), dma((N,)),
-        dma((K + 1,)), dma((K + 1,)), dma((Z,)), dma((Z,)), dma((2,)),
+        dma((7,)), dma((4,)), dma((8,)), dma((4,)), dma((4,)), dma((2, Z)),
+        dma((N, K)), dma((N,)), dma((Z, 2)), dma((Z, 2)), dma((N,)), dma((1,)), dma((half,)), dma((half, 2)),
+        dma((N,)), dma((Z, N, K)), dma((Z,)), dma((Z,)), dma((N,)), dma((K + 1,)), dma((Z,)),
     ]
     spec = pl.BlockSpec(memory_space=pltpu.VMEM)
     hbm = pl.BlockSpec(memory_space=pltpu.MemorySpace.HBM)

time: 70 us -> 68.4 us (0.977)
  Pallas kernels: 69.1 us -> 67.5 us
    pallas_call x1, Pallas kernels: 68 us -> 66.4 us  [body_fast(): pl.pallas_call(functools.partial(fast_kernel, M, N), out_shape=(jax.Shape...]
where the time goes in v5:
time: 68.4 us; the launch traced here: 68.3 us
  Pallas kernels  67.5 us (99%)
  between operations  0.8 us (1%)
    pallas_call x1, Pallas kernels, body_fast(): pl.pallas_call(functools.partial(fast_kernel, M, N), out_shape=(jax.Shape...  66.4 us

profile of v5, /device:TPU:0, one launch (start us, length us, event | category | flops | bytes accessed | tf_op | source)
XLA Modules:
  0.0 68.3 jit_solution(8796660692065770744)
XLA Ops:
  0.6 66.4 %shard_map.94 = (bf16[128,512]{1,0:T(8,128)(2,1)S(1)}, bf16[4,256,4,128]{3,2,1,0:T(4,128)(2,1)S(1)}, bf16[256,256]{1,0:T(8,128)(2,1)S(1)}) custom-call(bf16[128,2048]{1,0:T(8,128)(2,1)} %hid_hbm.1, bf16[4,512]{1,0:T(4,128)(2,1)} %mix_hbm.1, bf16[2048,4,512]{2,1,0:T(4,128)(2,1)} %proj_hbm.1, bf16[2048,256]{1,0:T(8,128)(2,1)} %vw_hbm.1, f32[4,128]{1,0:T(4,128)} %logz_hbm.1, ...), custom_call_target="tpu_custom_call" | custom-call | tf_op jit(solution)/shard_map/pallas_call | solution.py:936
  67.0 1.1 %shard_map.95 = (bf16[128,512]{1,0:T(8,128)(2,1)}, bf16[256,4,512]{2,1,0:T(4,128)(2,1)}, bf16[256,256]{1,0:T(8,128)(2,1)}) custom-call(bf16[128,512]{1,0:T(8,128)(2,1)S(1)} %get-tuple-element.6.hid, bf16[4,256,4,128]{3,2,1,0:T(4,128)(2,1)S(1)} %get-tuple-element.7.proj, bf16[256,256]{1,0:T(8,128)(2,1)S(1)} %get-tuple-element.8.voc), custom_call_target="tpu_custom_call" | custom-call | tf_op jit(solution)/shard_map/pallas_call | solution.py:953

commit v6 on v5

--- a/solution.py
+++ b/solution.py
@@ -363,15 +363,15 @@
 
 
 ORDER = (
-    (0, 0), (1, 0), (2, 0), (0, 1), (2, 1), (12,), (0, 2), (1, 1), (0, 3), (1, 3), (10, 2), (8,), (9,),
-    (1, 2), (3, 0, 1), (3, 0, 2), (3, 0, 3), (11, 3, 0), (3, 1, 1), (2, 3), (4, 0, 3), (4, 0, 1),
-    (3, 1, 2), (11, 3, 1), (2, 2), (10, 3), (5, 0, 0), (4, 0, 2), (4, 1, 1), (5, 2, 0), (13,), (5, 0, 1),
-    (4, 3, 1), (3, 1, 3), (3, 3, 2), (3, 3, 1), (6, 0, 1), (5, 0, 3), (6, 0, 0), (5, 0, 2), (4, 1, 2),
-    (5, 1, 0), (6, 0, 3), (6, 0, 2), (7, 0), (4, 1, 3), (4, 2, 1), (3, 3, 3), (5, 1, 1), (4, 3, 2),
-    (3, 2, 1), (5, 1, 2), (5, 1, 3), (3, 2, 2), (5, 3, 0), (6, 1, 0), (6, 1, 1), (5, 3, 1), (6, 1, 2),
-    (3, 2, 3), (4, 3, 3), (6, 1, 3), (7, 1), (6, 2, 0), (4, 2, 2), (6, 3, 1), (6, 3, 0), (5, 3, 2), (15,),
-    (4, 2, 3), (5, 3, 3), (6, 3, 2), (5, 2, 1), (5, 2, 2), (6, 3, 3), (7, 3), (5, 2, 3), (6, 2, 2),
-    (6, 2, 1), (6, 2, 3), (7, 2), (14, 0), (14, 1), (14, 2), (14, 3),
+    (0, 0), (1, 0), (2, 0), (0, 1), (0, 2), (1, 1), (1, 2), (2, 1), (0, 3), (12,), (8,), (3, 0, 1), (9,),
+    (1, 3), (10, 2), (3, 0, 2), (4, 0, 1), (11, 3, 1), (2, 2), (5, 0, 0), (3, 1, 1), (4, 0, 3), (11, 3, 0),
+    (5, 2, 0), (4, 0, 2), (3, 1, 2), (5, 1, 0), (6, 0, 0), (3, 0, 3), (2, 3), (5, 0, 1), (4, 2, 1),
+    (10, 3), (4, 1, 1), (3, 1, 3), (3, 2, 1), (5, 0, 3), (5, 0, 2), (6, 0, 1), (4, 1, 2), (5, 3, 0),
+    (3, 2, 2), (13,), (6, 2, 0), (3, 3, 1), (6, 0, 3), (6, 0, 2), (7, 0), (4, 1, 3), (4, 2, 2), (3, 2, 3),
+    (5, 1, 2), (5, 1, 1), (3, 3, 2), (6, 1, 0), (4, 3, 1), (5, 1, 3), (6, 1, 1), (6, 1, 2), (4, 2, 3),
+    (3, 3, 3), (6, 3, 0), (6, 1, 3), (7, 1), (5, 2, 1), (4, 3, 2), (5, 2, 2), (4, 3, 3), (5, 3, 1),
+    (6, 2, 1), (5, 2, 3), (6, 3, 1), (6, 2, 2), (5, 3, 2), (14, 2), (15,), (6, 2, 3), (5, 3, 3), (7, 2),
+    (6, 3, 2), (6, 3, 3), (7, 3), (14, 3), (14, 0), (14, 1),
 )
 
 
@@ -399,7 +399,7 @@
     vgb, vgy, vsum, vout, vin, hss, hsr, own_hs, acc, psend, precv, mgrad,
     l_sem, w_sem, all_s, over_s, own_s, on_s,
     ctx_r, mix_r, hz_r, hp_r, vx_r, vp_r, vwz_r, vwy_r,
-    tgt_r, lg_r, vy_r, vz_r, hs_r, pp_r, sc_r,
+    tgt_r, lg_r, ld_r, vy_r, vz_r, hs_r, pp_r, sc_r,
 ):
     K, D, E = w.shape
     T = hida.shape[2]
@@ -688,10 +688,10 @@
     def shares(zz, k):
         piece = lgall.at[zz, me_v, k]
         return [
-            remote(piece, piece, over_s.at[1], lg_r.at[zz, me_v, k],
+            remote(piece, piece, over_s.at[1], lg_r.at[zz, chip, k],
                    {"voc": lax.rem(chip + i, half) * 2 + core})
             for i in range(1, half)
-        ] + [remote(piece, piece, over_s.at[2], lg_r.at[zz, me_v, k], {"voc": partner})]
+        ] + [remote(piece, piece, over_s.at[2], ld_r.at[zz, k], {"voc": partner})]
 
     def share(zz, k):
         for c in shares(zz, k):
@@ -710,11 +710,11 @@
     @scoped
     def own_line(k):
         piece = lgall.at[z, me_v, k]
-        pl.when(has_r)(remote(piece, piece, own_s.at[0], lg_r.at[z, me_v, k], {"tok": me_t + 2}).start)
-        pl.when(has_l)(remote(piece, piece, own_s.at[1], lg_r.at[z, me_v, k], {"tok": me_t - 2}).start)
+        pl.when(has_r)(remote(piece, piece, own_s.at[0], lg_r.at[z, chip, k], {"tok": me_t + 2}).start)
+        pl.when(has_l)(remote(piece, piece, own_s.at[1], lg_r.at[z, chip, k], {"tok": me_t - 2}).start)
         if k == 0:
             for way, end in ((0, 0), (1, Z - 1)):
-                far = remote(piece, piece, own_s.at[2 + way], lg_r.at[z, me_v, k],
+                far = remote(piece, piece, own_s.at[2 + way], lg_r.at[z, chip, k],
                              {"tok": me_t + (1 - 2 * way) * (M - 2)})
                 pl.when(z == end)(far.start)
 
@@ -729,11 +729,11 @@
         if k == 0:
             there = near_end(zz, there, to)
         piece = lgall.at[zz, me_v, k]
-        on = remote(piece, piece, on_s.at[1 if k == 0 else 0, j], lg_r.at[zz, me_v, k], {"tok": to})
+        on = remote(piece, piece, on_s.at[1 if k == 0 else 0, j], lg_r.at[zz, chip, k], {"tok": to})
 
         @pl.when(there if fwd else jnp.logical_not(there))
         def _():
-            arrived(piece, lg_r.at[zz, me_v, k])
+            arrived(piece, lg_r.at[zz, chip, k])
             if fwd:
                 on.start()
             share(zz, k)
@@ -744,16 +744,14 @@
         for i in range(1, half):
             s = lax.rem(chip - i + half, half) * 2 + core
             piece = lgall.at[zz, s, k]
-            arrived(piece, lg_r.at[zz, s, k])
-            remote(piece, piece, over_s.at[3], lg_r.at[zz, s, k], {"voc": partner}).start()
+            arrived(piece, lg_r.at[zz, s // 2, k])
+            remote(piece, piece, over_s.at[3], ld_r.at[zz, k], {"voc": partner}).start()
 
     @scoped
     def pre_grad(k, j):
         zz = mate(j)
         rows = slice(k * T, (k + 1) * T)
-        for i in range(half):
-            s = lax.rem(chip + i, half) * 2 + 1 - core
-            arrived(lgall.at[zz, s, k], lg_r.at[zz, s, k])
+        arrived(lgall.at[zz, 0:half, k], ld_r.at[zz, k])
         total = None
         for s in range(N):
             part = jnp.dot(lgall[zz, s, k], vwt[s], preferred_element_type=F32)
@@ -814,12 +812,12 @@
         for k in range(K):
             rows = slice(k * T, (k + 1) * T)
             lg[rows, :] = (column(scale[z, k:k + 1, :], V) * logit[rows, :]).astype(BF16)
-        for s in range(N):
-            vgb[s * E:(s + 1) * E, :] = lax.dot_general(
-                ctx[s], lg[...], TN, preferred_element_type=F32).astype(BF16)
-            for zz in range(s * Z // N, (s + 1) * Z // N):
-                send(vgb.at[pl.ds((zz * 2 + 1 - y) * R, R)], vgy.at[zz], vy_r.at[zz],
-                     {"tok": ypart})
+        for part in range(0, N, half):
+            for s in range(part, part + half):
+                vgb[s * E:(s + 1) * E, :] = lax.dot_general(
+                    ctx[s], lg[...], TN, preferred_element_type=F32).astype(BF16)
+            for zz in range(part * Z // N, (part + half) * Z // N):
+                send(vgb.at[pl.ds((zz * 2 + 1 - y) * R, R)], vgy.at[zz], vy_r.at[zz], {"tok": ypart})
 
     @scoped
     def vw_done():
@@ -929,7 +927,7 @@
         vm((K, T), F32),
         dma((7,)), dma((4,)), dma((8,)), dma((4,)), dma((4,)), dma((2, Z)),
         dma((N, K)), dma((N,)), dma((Z, 2)), dma((Z, 2)), dma((N,)), dma((1,)), dma((half,)), dma((half, 2)),
-        dma((N,)), dma((Z, N, K)), dma((Z,)), dma((Z,)), dma((N,)), dma((K + 1,)), dma((Z,)),
+        dma((N,)), dma((Z, half, K)), dma((Z, K)), dma((Z,)), dma((Z,)), dma((N,)), dma((K + 1,)), dma((Z,)),
     ]
     spec = pl.BlockSpec(memory_space=pltpu.VMEM)
     hbm = pl.BlockSpec(memory_space=pltpu.MemorySpace.HBM)

time: 68.4 us -> 67.7 us (0.990)
  Pallas kernels: 67.5 us -> 66.8 us
    pallas_call x1, Pallas kernels: 66.4 us -> 65.7 us  [body_fast(): pl.pallas_call(functools.partial(fast_kernel, M, N), out_shape=(jax.Shape...]
where the time goes in v6:
time: 67.7 us; the launch traced here: 67.6 us
  Pallas kernels  66.8 us (99%)
  between operations  0.8 us (1%)
    pallas_call x1, Pallas kernels, body_fast(): pl.pallas_call(functools.partial(fast_kernel, M, N), out_shape=(jax.Shape...  65.7 us

profile of v6, /device:TPU:0, one launch (start us, length us, event | category | flops | bytes accessed | tf_op | source)
XLA Modules:
  0.0 67.6 jit_solution(9043442732353363511)
XLA Ops:
  0.6 65.7 %shard_map.94 = (bf16[128,512]{1,0:T(8,128)(2,1)S(1)}, bf16[4,256,4,128]{3,2,1,0:T(4,128)(2,1)S(1)}, bf16[256,256]{1,0:T(8,128)(2,1)S(1)}) custom-call(bf16[128,2048]{1,0:T(8,128)(2,1)} %hid_hbm.1, bf16[4,512]{1,0:T(4,128)(2,1)} %mix_hbm.1, bf16[2048,4,512]{2,1,0:T(4,128)(2,1)} %proj_hbm.1, bf16[2048,256]{1,0:T(8,128)(2,1)} %vw_hbm.1, f32[4,128]{1,0:T(4,128)} %logz_hbm.1, ...), custom_call_target="tpu_custom_call" | custom-call | tf_op jit(solution)/shard_map/pallas_call | solution.py:934
  66.3 1.1 %shard_map.95 = (bf16[128,512]{1,0:T(8,128)(2,1)}, bf16[256,4,512]{2,1,0:T(4,128)(2,1)}, bf16[256,256]{1,0:T(8,128)(2,1)}) custom-call(bf16[128,512]{1,0:T(8,128)(2,1)S(1)} %get-tuple-element.6.hid, bf16[4,256,4,128]{3,2,1,0:T(4,128)(2,1)S(1)} %get-tuple-element.7.proj, bf16[256,256]{1,0:T(8,128)(2,1)S(1)} %get-tuple-element.8.voc), custom_call_target="tpu_custom_call" | custom-call | tf_op jit(solution)/shard_map/pallas_call | solution.py:951

commit v7 on v6

--- a/solution.py
+++ b/solution.py
@@ -398,7 +398,7 @@
     ctx, ctxz, mix_all, htr, logit, lg, lgall, tgt, scale, pg,
     vgb, vgy, vsum, vout, vin, hss, hsr, own_hs, acc, psend, precv, mgrad,
     l_sem, w_sem, all_s, over_s, own_s, on_s,
-    ctx_r, mix_r, hz_r, hp_r, vx_r, vp_r, vwz_r, vwy_r,
+    ctx_r, ctd_r, mix_r, hz_r, hp_r, vx_r, vp_r, vwz_r, vwy_r,
     tgt_r, lg_r, ld_r, vy_r, vz_r, hs_r, pp_r, sc_r,
 ):
     K, D, E = w.shape
@@ -552,7 +552,7 @@
     for c in loads[3:]:
         c.wait()
     for d in range(1, N):
-        send(mix, mix_all.at[d], mix_r.at[d], {"voc": lax.rem(me_v + d, N)})
+        send(mix, mix_all.at[d], mix_r.at[0], {"voc": lax.rem(me_v + d, N)})
     send(vw.at[rows_of(partner, E)], vwe.at[me_v], vp_r.at[0], {"voc": partner})
     for c in range(chunks):
         unmix(c)
@@ -569,9 +569,9 @@
             vw_pass()
         piece = ctx.at[me_v, pl.ds(k * T, T)]
         for i in range(1, half):
-            send(piece, piece, ctx_r.at[me_v, k],
+            send(piece, piece, ctx_r.at[chip, k],
                  {"voc": lax.rem(chip + i, half) * 2 + core})
-        send(piece, piece, ctx_r.at[me_v, k], {"voc": partner})
+        send(piece, piece, ctd_r.at[chip], {"voc": partner})
 
     @scoped
     def add_logits(s, first=False):
@@ -584,7 +584,7 @@
         there, to = onward(zz)
         piece = hid_piece(zz, core, p)
         on = remote(piece, piece, on_s.at[0, j], hz_r.at[zz, p], {"tok": to})
-        over = remote(piece, piece, over_s.at[0], hp_r.at[zz, p], {"voc": partner})
+        over = remote(piece, piece, over_s.at[0], hp_r.at[zz], {"voc": partner})
 
         @pl.when(there if fwd else jnp.logical_not(there))
         def _():
@@ -597,8 +597,7 @@
     def ctx_mate(j, ks):
         zz = mate(j)
         if ks[0] == 0:
-            for p in range(2):
-                arrived(hid_piece(zz, 1 - core, p), hp_r.at[zz, p])
+            arrived(hida.at[zz, 1 - core], hp_r.at[zz])
         for k in ks:
             ctxz[zz, k * T:(k + 1) * T, :] = context(zz, k)
 
@@ -607,22 +606,20 @@
         for i in range(1, half):
             s = lax.rem(chip - i + half, half) * 2 + core
             piece = ctx.at[s, pl.ds(k * T, T)]
-            arrived(piece, ctx_r.at[s, k])
-            send(piece, piece, ctx_r.at[s, k], {"voc": partner})
+            arrived(piece, ctx_r.at[s // 2, k])
+            send(piece, piece, ctd_r.at[s // 2], {"voc": partner})
 
     add_logits(me_v, True)
     for j in range(1, min(Z, 3)):
         relay_hid(j, 0, True)
-    for k in range(K):
-        arrived(ctx.at[partner, pl.ds(k * T, T)], ctx_r.at[partner, k])
+    arrived(ctx.at[partner], ctd_r.at[chip])
     add_logits(partner)
 
     tcol = column(targets[...].astype(F32), V)
     ids = (me_v * V + lax.broadcasted_iota(jnp.int32, (T, V), 1)).astype(F32)
     onehot = (tcol == ids).astype(F32)
     mix_all[0] = mix[...]
-    for d in range(1, N):
-        arrived(mix_all.at[d], mix_r.at[d])
+    arrived(mix_all.at[1:N], mix_r.at[0])
     mixing = jnp.zeros((K, T), F32)
     for d in range(N):
         s = lax.rem(me_v - d + N, N)
@@ -658,8 +655,7 @@
         add_logits(lax.rem(chip - i + half, half) * 2 + core)
     for i in range(1, half):
         s = lax.rem(chip - i + half, half) * 2 + 1 - core
-        for k in range(K):
-            arrived(ctx.at[s, pl.ds(k * T, T)], ctx_r.at[s, k])
+        arrived(ctx.at[s], ctd_r.at[s // 2])
         add_logits(s)
 
     lane = lax.broadcasted_iota(jnp.int32, (T, 128), 1)
@@ -669,11 +665,10 @@
         table = jnp.where(lane == k, part, table)
     tgt[0] = table.T[0:8, :]
     for d in range(1, N):
-        send(tgt.at[0], tgt.at[d], tgt_r.at[d], {"voc": lax.rem(me_v + d, N)})
+        send(tgt.at[0], tgt.at[d], tgt_r.at[0], {"voc": lax.rem(me_v + d, N)})
     @scoped
     def scales():
-        for d in range(1, N):
-            arrived(tgt.at[d], tgt_r.at[d])
+        arrived(tgt.at[1:N], tgt_r.at[0])
         target = tgt[0]
         for d in range(1, N):
             target = target + tgt[d]
@@ -926,8 +921,8 @@
         vm((T, E), F32), vm((K, R, E), F32), vm((K, R, E), BF16), vm((K, R, E), BF16),
         vm((K, T), F32),
         dma((7,)), dma((4,)), dma((8,)), dma((4,)), dma((4,)), dma((2, Z)),
-        dma((N, K)), dma((N,)), dma((Z, 2)), dma((Z, 2)), dma((N,)), dma((1,)), dma((half,)), dma((half, 2)),
-        dma((N,)), dma((Z, half, K)), dma((Z, K)), dma((Z,)), dma((Z,)), dma((N,)), dma((K + 1,)), dma((Z,)),
+        dma((half, K)), dma((half,)), dma((1,)), dma((Z, 2)), dma((Z,)), dma((N,)), dma((1,)), dma((half,)), dma((half, 2)),
+        dma((1,)), dma((Z, half, K)), dma((Z, K)), dma((Z,)), dma((Z,)), dma((N,)), dma((K + 1,)), dma((Z,)),
     ]
     spec = pl.BlockSpec(memory_space=pltpu.VMEM)
     hbm = pl.BlockSpec(memory_space=pltpu.MemorySpace.HBM)

time: 67.7 us -> 67.6 us (level)
  no operation moved by 1% of the time
where the time goes in v7:
time: 67.6 us; the launch traced here: 67.4 us
  Pallas kernels  66.6 us (99%)
  between operations  0.8 us (1%)
    pallas_call x1, Pallas kernels, body_fast(): pl.pallas_call(functools.partial(fast_kernel, M, N), out_shape=(jax.Shape...  65.5 us

profile of v7, /device:TPU:0, one launch (start us, length us, event | category | flops | bytes accessed | tf_op | source)
XLA Modules:
  0.0 67.4 jit_solution(9587946110628643730)
XLA Ops:
  0.6 65.5 %shard_map.94 = (bf16[128,512]{1,0:T(8,128)(2,1)S(1)}, bf16[4,256,4,128]{3,2,1,0:T(4,128)(2,1)S(1)}, bf16[256,256]{1,0:T(8,128)(2,1)S(1)}) custom-call(bf16[128,2048]{1,0:T(8,128)(2,1)} %hid_hbm.1, bf16[4,512]{1,0:T(4,128)(2,1)} %mix_hbm.1, bf16[2048,4,512]{2,1,0:T(4,128)(2,1)} %proj_hbm.1, bf16[2048,256]{1,0:T(8,128)(2,1)} %vw_hbm.1, f32[4,128]{1,0:T(4,128)} %logz_hbm.1, ...), custom_call_target="tpu_custom_call" | custom-call | tf_op jit(solution)/shard_map/pallas_call | solution.py:929
  66.2 1.1 %shard_map.95 = (bf16[128,512]{1,0:T(8,128)(2,1)}, bf16[256,4,512]{2,1,0:T(4,128)(2,1)}, bf16[256,256]{1,0:T(8,128)(2,1)}) custom-call(bf16[128,512]{1,0:T(8,128)(2,1)S(1)} %get-tuple-element.6.hid, bf16[4,256,4,128]{3,2,1,0:T(4,128)(2,1)S(1)} %get-tuple-element.7.proj, bf16[256,256]{1,0:T(8,128)(2,1)S(1)} %get-tuple-element.8.voc), custom_call_target="tpu_custom_call" | custom-call | tf_op jit(solution)/shard_map/pallas_call | solution.py:946
